TPU v7x, 32 devices: a whole 2x2x4 slice. The times are simulated.
32 devices in a mesh: seq: 8 (over y, x, core), dp: 4 (over z).
Axes of the slice: x: 2, y: 2, z: 4, core: 2. Of those that a mesh axis runs over, the one named last changes fastest.
Arguments:
- queries: bfloat16 [4, 3072, 2048], P('dp', 'seq'), may hold values from -40 to 40
- keys: bfloat16 [4, 3072, 2048], P('dp', 'seq'), may hold values from -40 to 40
- values: bfloat16 [4, 3072, 2048], P('dp', 'seq'), may hold values from -6 to 6
- out_grad: bfloat16 [4, 3072, 2048], P('dp', 'seq'), may hold values from -6 to 6
- proj_weight: bfloat16 [2048, 2048], P('dp'), may hold values from -0.125 to 0.125
- lengths: int32 [4], P('dp'), may hold values from 768 to 3072
Outputs:
- query_grad: bfloat16 [4, 3072, 2048], P('dp', 'seq')
- key_grad: bfloat16 [4, 3072, 2048], P('dp', 'seq')
- value_grad: bfloat16 [4, 3072, 2048], P('dp', 'seq')
- weight_grad: float32 [2048, 2048], P('dp', 'seq')
All inputs are finite; a program needn't handle non-finite values.
Results may differ from a plain program's by a relative error of at most 0.019.
Values may be sent and summed in bfloat16 or wider, within the bound.
A program may use at most 192 MiB of HBM per device.

v0:
```python
import jax
import jax.numpy as jnp
from jax import lax
from jax.sharding import PartitionSpec as P

HEAD_DIM = 128
CYCLE = 2


def from_behind(block, axis, distance):
    devices = range(lax.axis_size(axis))
    route = [(i - distance, i) for i in devices if i - distance in devices]
    return lax.ppermute(block, axis, route)


def per_device(queries, keys, values, out_grad, proj_weight, lengths):
    scale = HEAD_DIM ** (-0.5)
    query_rows = queries[0]
    key_rows = keys[0]
    value_rows = values[0]
    grad_rows = out_grad[0]
    tokens = query_rows.shape[0]
    width = query_rows.shape[1]
    heads = width // HEAD_DIM
    position = lax.axis_index("seq")
    query_pos = position * tokens + jnp.arange(tokens, dtype=jnp.int32)
    live = (query_pos < lengths[0]).astype(jnp.bfloat16)
    grad_masked = grad_rows * live[:, None]
    out_bwd = lax.dot_general(
        grad_masked,
        lax.all_gather(proj_weight, "dp", axis=0, tiled=True),
        (((1,), (1,)), ((), ())),
        preferred_element_type=jnp.float32,
    ).astype(jnp.bfloat16)
    blocks = [(key_rows, value_rows)]
    for offset in range(1, CYCLE + 1):
        blocks.append(from_behind((key_rows, value_rows), "seq", offset))
    query_heads = query_rows.reshape(tokens, heads, HEAD_DIM)
    causal = jnp.arange(tokens)[:, None] >= jnp.arange(tokens)[None, :]
    score_list = []
    for offset in range(CYCLE + 1):
        key_heads = blocks[offset][0].reshape(tokens, heads, HEAD_DIM)
        scores = (
            jnp.einsum("thd,shd->hts", query_heads, key_heads, preferred_element_type=jnp.float32)
            * scale
        )
        if offset == 0:
            scores = jnp.where(causal[None], scores, -1e30)
        else:
            scores = jnp.where(position >= offset, scores, -1e30)
        score_list.append(scores)
    maximum = score_list[0].max(axis=2, keepdims=True)
    for scores in score_list[1:]:
        maximum = jnp.maximum(maximum, scores.max(axis=2, keepdims=True))
    total = jnp.zeros_like(maximum)
    for scores in score_list:
        total = total + jnp.sum(jnp.exp(scores - maximum), axis=2, keepdims=True)
    lse = maximum + jnp.log(total)
    prob_list = []
    attn_sum = jnp.zeros((tokens, heads, HEAD_DIM), jnp.float32)
    for offset in range(CYCLE + 1):
        probs = jnp.exp(score_list[offset] - lse)
        probs_b = probs.astype(jnp.bfloat16)
        prob_list.append((probs, probs_b))
        value_heads = blocks[offset][1].reshape(tokens, heads, HEAD_DIM)
        attn_sum = attn_sum + jnp.einsum(
            "hts,shd->thd", probs_b, value_heads, preferred_element_type=jnp.float32
        )
    attn_out = attn_sum.astype(jnp.bfloat16)
    out_heads = out_bwd.reshape(tokens, heads, HEAD_DIM)
    delta = jnp.sum(out_heads.astype(jnp.float32) * attn_out.astype(jnp.float32), axis=2)
    delta_rows = delta.T[:, :, None]
    query_accum = jnp.zeros((tokens, heads, HEAD_DIM), jnp.float32)
    key_accum = jnp.zeros((tokens, width), jnp.float32)
    value_accum = jnp.zeros((tokens, width), jnp.float32)
    for offset in range(CYCLE + 1):
        key_heads = blocks[offset][0].reshape(tokens, heads, HEAD_DIM)
        value_heads = blocks[offset][1].reshape(tokens, heads, HEAD_DIM)
        probs, probs_b = prob_list[offset]
        prob_grad = jnp.einsum(
            "thd,shd->hts", out_heads, value_heads, preferred_element_type=jnp.float32
        )
        score_grad = (probs * (prob_grad - delta_rows) * scale).astype(jnp.bfloat16)
        query_accum = query_accum + jnp.einsum(
            "hts,shd->thd", score_grad, key_heads, preferred_element_type=jnp.float32
        )
        key_term = (
            jnp.einsum("hts,thd->shd", score_grad, query_heads, preferred_element_type=jnp.float32)
            .astype(jnp.bfloat16)
            .reshape(tokens, width)
        )
        value_term = (
            jnp.einsum("hts,thd->shd", probs_b, out_heads, preferred_element_type=jnp.float32)
            .astype(jnp.bfloat16)
            .reshape(tokens, width)
        )
        if offset > 0:
            key_term, value_term = from_behind((key_term, value_term), "seq", -offset)
        key_accum = key_accum + key_term.astype(jnp.float32)
        value_accum = value_accum + value_term.astype(jnp.float32)
    attn_flat = attn_out.reshape(tokens, width)
    whole_term = lax.dot_general(
        attn_flat, grad_masked, (((0,), (0,)), ((), ())), preferred_element_type=jnp.float32
    )
    column_sums = lax.psum_scatter(whole_term, "seq", scatter_dimension=1, tiled=True)
    weight_grad = lax.psum_scatter(column_sums, "dp", scatter_dimension=0, tiled=True)
    query_grad = query_accum.reshape(tokens, width).astype(jnp.bfloat16)
    return (
        query_grad[None],
        key_accum.astype(jnp.bfloat16)[None],
        value_accum.astype(jnp.bfloat16)[None],
        weight_grad,
    )


def solution(mesh):
    placed = (
        P("dp", "seq", None),
        P("dp", "seq", None),
        P("dp", "seq", None),
        P("dp", "seq", None),
        P("dp", None),
        P("dp"),
    )
    return jax.shard_map(
        per_device,
        mesh=mesh,
        in_specs=placed,
        out_specs=(
            P("dp", "seq", None),
            P("dp", "seq", None),
            P("dp", "seq", None),
            P("dp", "seq"),
        ),
        check_vma=False,
    )
```

profile of v0, /device:TPU:0, one launch (start us, length us, event | category | flops | bytes accessed | tf_op | source)
XLA Modules:
  0.0 448.5 jit_solution(16561103220020566082)
XLA Ops:
  7.2 0.0 all-gather.2.cloned.1.call-start
  7.2 0.7 all-gather.2.cloned.1.call-update
  7.9 0.0 reduce-scatter.3.cloned.1.call-start
  8.0 6.1 %collective-permute-start.3 = (bf16[384,2048]{1,0:T(8,128)(2,1)}, bf16[384,2048]{1,0:T(8,128)(2,1)}, u32[]{:S(2)}, u32[]{:S(2)}) collective-permute-start(bf16[384,2048]{1,0:T(8,128)(2,1)} %bitcast.109), channel_id=1, source_target_pairs={{0,8},{4,12},{8,16},{12,20},{16,24},{20,28},{1,9},{5,13},{9,17},{1... | collective-permute-start | bytes 4718600 | tf_op jit(solution)/shard_map/ppermute | solution.py:13
  14.1 2.6 collective-permute-start.2
  16.7 0.9 copy.120
  17.5 2.8 collective-permute-start
  20.3 3.5 collective-permute-start.1
  23.8 2.7 copy.123
  27.1 1.9 copy.121
  29.1 5.4 %fusion.3 = (f32[16,384]{1,0:T(8,128)S(1)}, f32[16,384,384]{1,2,0:T(8,128)}) fusion(pred[384,384]{0,1:T(8,128)(4,1)S(1)} %iota_compare_fusion, bf16[384,16,128]{0,2,1:T(8,128)(2,1)S(1)} %bitcast.81, bf16[384,16,128]{0,2,1:T(8,128)(2,1)S(1)} %bitcast.93), kind=kOutput, calls=%fused_computation.15 | convolution fusion | flops 611051520 | bytes 12754944 | tf_op jit(solution)/shard_map/thd,shd->hts/dot_general | solution.py:44
  34.5 13.5 %collective-permute-done.3 = bf16[384,2048]{1,0:T(8,128)(2,1)} collective-permute-done((bf16[384,2048]{1,0:T(8,128)(2,1)}, bf16[384,2048]{1,0:T(8,128)(2,1)}, u32[]{:S(2)}, u32[]{:S(2)}) %collective-permute-start.3) | collective-permute-done | bytes 1572896 | tf_op jit(solution)/shard_map/ppermute | solution.py:13
  47.9 2.6 copy.69
  50.5 0.0 collective-permute-done.2
  50.5 2.6 copy.67
  53.1 0.0 collective-permute-done
  53.1 3.1 fusion.4
  56.2 25.3 %collective-permute-done.1 = bf16[384,2048]{0,1:T(8,128)(2,1)} collective-permute-done((bf16[384,2048]{0,1:T(8,128)(2,1)S(1)}, bf16[384,2048]{0,1:T(8,128)(2,1)}, u32[]{:S(2)}, u32[]{:S(2)}) %collective-permute-start.1) | collective-permute-done | bytes 1572896 | tf_op jit(solution)/shard_map/ppermute | solution.py:13
  81.5 3.0 fusion.5
  84.6 6.1 %exponential_reduce_fusion.1 = (f32[16,384]{1,0:T(8,128)S(1)}, f32[16,384]{1,0:T(8,128)S(1)}, f32[16,384]{1,0:T(8,128)S(1)}) fusion(f32[16,384,384]{1,2,0:T(8,128)S(1)} %get-tuple-element.20, f32[16,384]{1,0:T(8,128)S(1)} %maximum_maximum_fusion, pred[]{:T(512)S(6)} %ge.26, f32[16,384,384]{1,2,0:T(8,128)S(1)} %get-tuple-element.16, pred[]{:T(512)S(6)} %ge.27, ...), kind=kLoop, calls=%fused_computation.7 | loop fusion | flops 28293120 | bytes 28557314 | tf_op jit(solution)/shard_map/reduce_sum | solution.py:57
  90.8 4.0 fusion.18
  94.8 4.4 fusion.21
  99.3 62.7 %all-gather.2.cloned.1.call-done = bf16[2048,2048]{1,0:T(8,128)(2,1)} async-done(((bf16[512,2048]{1,0:T(8,128)(2,1)}), bf16[2048,2048]{1,0:T(8,128)(2,1)}) %all-gather.2.cloned.1.call-update) | async-done | bytes 8388624 | tf_op jit(solution)/shard_map/all_gather | solution.py:31
  161.9 8.5 %convolution_convert_fusion = bf16[384,2048]{1,0:T(8,128)(2,1)} fusion(bf16[2048,2048]{1,0:T(8,128)(2,1)} %all-gather.2.cloned.1.call-done, bf16[1,384,2048]{2,1,0:T(8,128)(2,1)} %param.9, bf16[384]{0:T(512)(128)(2,1)S(1)} %fusion.23), kind=kOutput, calls=%fused_computation.23 | convolution fusion | flops 3222798336 | bytes 11535104 | tf_op jit(solution)/shard_map/dot_general | solution.py:29
  170.4 2.6 copy.122
  173.0 9.3 %multiply_reduce_fusion = (f32[384,16]{0,1:T(8,128)S(1)}, bf16[16,384,128]{1,2,0:T(8,128)(2,1)S(1)}) fusion(bf16[384,2048]{0,1:T(8,128)(2,1)} %copy.122, bf16[384,16,128]{0,2,1:T(8,128)(2,1)} %bitcast.97, f32[16,384,384]{1,2,0:T(8,128)} %copy-done, f32[16,384]{1,0:T(8,128)S(1)} %log_add_fusion, pred[]{:T(512)S(6)} %ge.27, f32[16,384,128]{1,2,0:T(8,128)} %fusion.21, ...), kind=kOutput, calls=%fused_computation.21 | convolution fusion | flops 618915840 | bytes 20496384 | tf_op jit(solution)/shard_map/hts,shd->thd/dot_general | solution.py:66
  182.3 8.1 %fusion.10 = f32[2048,2048]{1,0:T(8,128)} fusion(bf16[384,2048]{0,1:T(8,128)(2,1)S(1)} %bitcast.96, bf16[1,384,2048]{2,1,0:T(8,128)(2,1)S(1)} %copy-done.7, bf16[384]{0:T(512)(128)(2,1)S(1)} %fusion.23), kind=kOutput, calls=%fused_computation.34 | convolution fusion | flops 3222011904 | bytes 19923712 | tf_op jit(solution)/shard_map/dot_general | solution.py:102
  190.4 0.0 reduce-scatter.3.cloned.1.call-update
  190.4 0.3 reduce-scatter.5.cloned.1.call-start
  190.7 8.2 %convolution_convert_fusion.2 = bf16[16,128,384]{2,1,0:T(8,128)(2,1)} fusion(bf16[384,16,128]{0,2,1:T(8,128)(2,1)} %bitcast.99, f32[16,384,384]{1,2,0:T(8,128)} %copy-done.1, f32[16,384]{1,0:T(8,128)S(1)} %log_add_fusion, pred[]{:T(512)S(6)} %ge.26), kind=kOutput, calls=%fused_computation.25 | convolution fusion | flops 614203392 | bytes 12607489 | tf_op jit(solution)/shard_map/hts,thd->shd/dot_general | solution.py:93
  198.9 2.9 copy.95
  201.8 9.4 %convolution_convert_fusion.1 = bf16[16,128,384]{2,1,0:T(8,128)(2,1)} fusion(bf16[384,16,128]{0,2,1:T(8,128)(2,1)} %bitcast.100, f32[16,384,384]{1,2,0:T(8,128)} %copy-done, f32[16,384]{1,0:T(8,128)S(1)} %log_add_fusion, pred[]{:T(512)S(6)} %ge.27), kind=kOutput, calls=%fused_computation.24 | convolution fusion | flops 614203392 | bytes 12607489 | tf_op jit(solution)/shard_map/hts,thd->shd/dot_general | solution.py:93
  211.2 2.8 copy.99
  214.0 1.3 collective-permute-start.7
  215.3 1.3 collective-permute-start.6
  216.6 8.3 %fusion.7 = f32[16,128,384]{2,1,0:T(8,128)} fusion(bf16[384,16,128]{0,2,1:T(8,128)(2,1)} %bitcast.101, f32[16,384,384]{1,2,0:T(8,128)} %get-tuple-element.18, f32[16,384]{1,0:T(8,128)S(1)} %log_add_fusion, pred[384,384]{0,1:T(8,128)(4,1)S(1)} %iota_compare_fusion), kind=kOutput, calls=%fused_computation.31 | convolution fusion | flops 614989824 | bytes 14327808 | tf_op jit(solution)/shard_map/hts,thd->shd/dot_general | solution.py:93
  225.0 4.0 copy.96
  229.0 7.8 %multiply_convert_fusion = bf16[16,384,384]{1,2,0:T(8,128)(2,1)S(1)} fusion(f32[16,384,384]{1,2,0:T(8,128)} %copy-done, f32[16,384]{1,0:T(8,128)S(1)} %bitcast.117, f32[16,384]{1,0:T(8,128)S(1)} %log_add_fusion, pred[]{:T(512)S(6)} %ge.27, bf16[384,16,128]{0,2,1:T(8,128)(2,1)} %bitcast.102, bf16[384,16,128]{0,2,1:T(8,128)(2,1)} %bitcast.98), kind=kOutput, calls=%fused_computation | convolution fusion | flops 620494848 | bytes 17350656 | tf_op jit(solution)/shard_map/thd,shd->hts/dot_general | solution.py:80
  236.7 2.8 convolution_convert_fusion.4
  239.5 2.7 copy.90
  242.3 8.0 %multiply_convert_fusion.1 = bf16[16,384,384]{1,2,0:T(8,128)(2,1)S(1)} fusion(f32[16,384,384]{1,2,0:T(8,128)} %copy-done.1, f32[16,384]{1,0:T(8,128)S(1)} %bitcast.118, f32[16,384]{1,0:T(8,128)S(1)} %log_add_fusion, pred[]{:T(512)S(6)} %ge.26, bf16[384,16,128]{0,2,1:T(8,128)(2,1)} %bitcast.103, bf16[384,16,128]{0,2,1:T(8,128)(2,1)} %bitcast.113), kind=kOutput, calls=%fused_computation.1 | convolution fusion | flops 620494848 | bytes 17350656 | tf_op jit(solution)/shard_map/thd,shd->hts/dot_general | solution.py:80
  250.3 2.8 convolution_convert_fusion.5
  253.1 2.7 copy.86
  255.7 1.3 collective-permute-start.4
  257.0 1.3 collective-permute-start.5
  258.3 136.9 %reduce-scatter.3.cloned.1.call-done = f32[2048,256]{1,0:T(8,128)} async-done(((f32[2048,2048]{1,0:T(8,128)}), f32[2048,256]{1,0:T(8,128)}) %reduce-scatter.3.cloned.1.call-update) | async-done | bytes 2097168 | tf_op jit(solution)/shard_map/reduce_scatter | solution.py:105
  395.2 0.0 reduce-scatter.5.cloned.1.call-update
  395.2 0.0 copy-start.6
  395.3 0.0 slice-start.3
  395.3 4.2 fusion.37
  399.5 0.0 slice-start.4
  399.5 6.2 %multiply_convert_fusion.2 = bf16[16,384,384]{1,2,0:T(8,128)(2,1)S(1)} fusion(f32[16,384,384]{1,2,0:T(8,128)} %get-tuple-element.18, f32[16,384]{1,0:T(8,128)S(1)} %bitcast.119, f32[16,384]{1,0:T(8,128)S(1)} %log_add_fusion, pred[384,384]{0,1:T(8,128)(4,1)S(1)} %iota_compare_fusion, bf16[384,16,128]{0,2,1:T(8,128)(2,1)S(1)} %bitcast.104, ...), kind=kOutput, calls=%fused_computation.2 | convolution fusion | flops 620494848 | bytes 17498112 | tf_op jit(solution)/shard_map/thd,shd->hts/dot_general | solution.py:80
  405.7 1.2 fusion.36
  406.9 0.9 copy-done.3
  407.8 2.7 add_convert_fusion.2
  410.5 1.6 copy.100
  412.2 5.5 %fusion.6 = f32[16,384,128]{1,2,0:T(8,128)} fusion(bf16[16,384,384]{1,2,0:T(8,128)(2,1)} %copy-done.3, bf16[384,16,128]{0,2,1:T(8,128)(2,1)S(1)} %bitcast.86), kind=kOutput, calls=%fused_computation.30 | convolution fusion | flops 605552640 | bytes 9437184 | tf_op jit(solution)/shard_map/hts,thd->shd/dot_general | solution.py:88
  417.7 3.5 copy.87
  421.2 0.0 collective-permute-done.7
  421.3 0.0 collective-permute-done.6
  421.3 4.9 %fusion.9 = bf16[1,384,2048]{2,1,0:T(8,128)(2,1)} fusion(bf16[384,2048]{1,0:T(8,128)(2,1)} %collective-permute-done.7, f32[384,2048]{1,0:T(8,128)} %copy.96, bf16[384,2048]{1,0:T(8,128)(2,1)} %collective-permute-done.6), kind=kLoop, calls=%fused_computation.33 | loop fusion | flops 3932160 | bytes 7864320 | tf_op jit(solution)/shard_map/broadcast_in_dim | solution.py:111
  426.2 0.0 collective-permute-done.4
  426.2 3.8 fusion.8
  430.0 11.7 %reduce-scatter.5.cloned.1.call-done = f32[512,256]{1,0:T(8,128)} async-done(((f32[2048,256]{1,0:T(8,128)}), f32[512,256]{1,0:T(8,128)}) %reduce-scatter.5.cloned.1.call-update) | async-done | bytes 524304 | tf_op jit(solution)/shard_map/reduce_scatter | solution.py:106
  (37 shorter events, 0.1 us)
Async XLA Ops:
  7.2 9.5 %copy-start.8 = (bf16[1,384,2048]{2,1,0:T(8,128)(2,1)S(1)}, bf16[1,384,2048]{2,1,0:T(8,128)(2,1)}, u32[]{:S(2)}) copy-start(bf16[1,384,2048]{2,1,0:T(8,128)(2,1)} %param.7) | copy-start | bytes 4718596
  7.2 154.7 %all-gather.2.cloned.1.call-start = ((), (), s32[]{:S(2)}) async-start(), calls=%async_computation.2 | async-start | bytes 10485760 | tf_op jit(solution)/shard_map/all_gather | solution.py:31
  7.9 387.3 %reduce-scatter.3.cloned.1.call-start = ((), (), s32[]{:S(2)}) async-start(), calls=%async_computation.3 | async-start | bytes 18874368 | tf_op jit(solution)/shard_map/reduce_scatter | solution.py:105
  8.0 40.0 %collective-permute-start.3 = (bf16[384,2048]{1,0:T(8,128)(2,1)}, bf16[384,2048]{1,0:T(8,128)(2,1)}, u32[]{:S(2)}, u32[]{:S(2)}) collective-permute-start(bf16[384,2048]{1,0:T(8,128)(2,1)} %bitcast.109), channel_id=1, source_target_pairs={{0,8},{4,12},{8,16},{12,20},{16,24},{20,28},{1,9},{5,13},{9,17},{1... | collective-permute-start | bytes 4718600 | tf_op jit(solution)/shard_map/ppermute | solution.py:13
  14.1 36.4 %collective-permute-start.2 = (bf16[384,2048]{1,0:T(8,128)(2,1)}, bf16[384,2048]{1,0:T(8,128)(2,1)}, u32[]{:S(2)}, u32[]{:S(2)}) collective-permute-start(bf16[384,2048]{1,0:T(8,128)(2,1)} %bitcast.110), channel_id=1, source_target_pairs={{0,4},{4,8},{8,12},{12,16},{16,20},{20,24},{24,28},{1,5},{5,9},{9,... | collective-permute-start | bytes 4718600 | tf_op jit(solution)/shard_map/ppermute | solution.py:13
  17.5 35.5 %collective-permute-start = (bf16[384,2048]{0,1:T(8,128)(2,1)S(1)}, bf16[384,2048]{0,1:T(8,128)(2,1)}, u32[]{:S(2)}, u32[]{:S(2)}) collective-permute-start(bf16[384,2048]{0,1:T(8,128)(2,1)S(1)} %bitcast.91), channel_id=1, source_target_pairs={{0,4},{4,8},{8,12},{12,16},{16,20},{20,24},{24,28},{1,5},{5,9},{9,... | collective-permute-start | bytes 4718600 | tf_op jit(solution)/shard_map/ppermute | solution.py:13
  20.3 61.2 %collective-permute-start.1 = (bf16[384,2048]{0,1:T(8,128)(2,1)S(1)}, bf16[384,2048]{0,1:T(8,128)(2,1)}, u32[]{:S(2)}, u32[]{:S(2)}) collective-permute-start(bf16[384,2048]{0,1:T(8,128)(2,1)S(1)} %bitcast.92), channel_id=1, source_target_pairs={{0,8},{4,12},{8,16},{12,20},{16,24},{20,28},{1,9},{5,13},{9,17},{1... | collective-permute-start | bytes 4718600 | tf_op jit(solution)/shard_map/ppermute | solution.py:13
  53.1 31.5 %slice-start = ((s8[9437184]{0:T(1024)(128)(4,1)}), s8[4194304]{0:T(1024)(128)(4,1)S(1)}, s32[]{:S(2)}) async-start(s8[9437184]{0:T(1024)(128)(4,1)} %bitcast.87), calls=%async_computation.5 | async-start | bytes 8388608
  53.1 31.5 %slice-start.1 = ((s8[9437184]{0:T(1024)(128)(4,1)}), s8[4194304]{0:T(1024)(128)(4,1)S(1)}, s32[]{:S(2)}) async-start(s8[9437184]{0:T(1024)(128)(4,1)} %bitcast.87), calls=%async_computation.6 | async-start | bytes 8388608
  56.2 34.6 %copy-start.1 = (f32[16,384,384]{1,2,0:T(8,128)}, f32[16,384,384]{1,2,0:T(8,128)S(1)}, u32[]{:S(2)}) copy-start(f32[16,384,384]{1,2,0:T(8,128)S(1)} %get-tuple-element.20) | copy-start | bytes 28311556
  81.5 3.1 slice-start.2
  84.6 6.2 %copy-start = (f32[16,384,384]{1,2,0:T(8,128)}, f32[16,384,384]{1,2,0:T(8,128)S(1)}, u32[]{:S(2)}) copy-start(f32[16,384,384]{1,2,0:T(8,128)S(1)} %get-tuple-element.16) | copy-start | bytes 28311556
  84.6 6.2 %copy-start.11 = (bf16[384,2048]{0,1:T(8,128)(2,1)S(1)}, bf16[384,2048]{0,1:T(8,128)(2,1)}, u32[]{:S(2)}) copy-start(bf16[384,2048]{0,1:T(8,128)(2,1)} %copy.67) | copy-start | bytes 4718596
  90.8 4.0 copy-start.9
  173.0 9.3 %copy-start.7 = (bf16[1,384,2048]{2,1,0:T(8,128)(2,1)S(1)}, bf16[1,384,2048]{2,1,0:T(8,128)(2,1)}, u32[]{:S(2)}) copy-start(bf16[1,384,2048]{2,1,0:T(8,128)(2,1)} %param.9) | copy-start | bytes 4718596
  190.4 251.3 %reduce-scatter.5.cloned.1.call-start = ((), (), s32[]{:S(2)}) async-start(), calls=%async_computation.4 | async-start | bytes 2621440 | tf_op jit(solution)/shard_map/reduce_scatter | solution.py:106
  214.0 207.2 %collective-permute-start.7 = (bf16[384,2048]{1,0:T(8,128)(2,1)}, bf16[384,2048]{1,0:T(8,128)(2,1)}, u32[]{:S(2)}, u32[]{:S(2)}) collective-permute-start(bf16[384,2048]{1,0:T(8,128)(2,1)} %copy.99), channel_id=1, source_target_pairs={{8,0},{12,4},{16,8},{20,12},{24,16},{28,20},{9,1},{13,5},{17,9},{2... | collective-permute-start | bytes 4718600 | tf_op jit(solution)/shard_map/ppermute | solution.py:13
  215.3 205.9 %collective-permute-start.6 = (bf16[384,2048]{1,0:T(8,128)(2,1)}, bf16[384,2048]{1,0:T(8,128)(2,1)}, u32[]{:S(2)}, u32[]{:S(2)}) collective-permute-start(bf16[384,2048]{1,0:T(8,128)(2,1)} %copy.95), channel_id=1, source_target_pairs={{4,0},{8,4},{12,8},{16,12},{20,16},{24,20},{28,24},{5,1},{9,5},{13... | collective-permute-start | bytes 4718600 | tf_op jit(solution)/shard_map/ppermute | solution.py:13
  236.7 2.8 copy-start.2
  250.3 2.8 copy-start.4
  255.7 170.5 %collective-permute-start.4 = (bf16[384,2048]{1,0:T(8,128)(2,1)}, bf16[384,2048]{1,0:T(8,128)(2,1)}, u32[]{:S(2)}, u32[]{:S(2)}) collective-permute-start(bf16[384,2048]{1,0:T(8,128)(2,1)} %copy.86), channel_id=1, source_target_pairs={{4,0},{8,4},{12,8},{16,12},{20,16},{24,20},{28,24},{5,1},{9,5},{13... | collective-permute-start | bytes 4718600 | tf_op jit(solution)/shard_map/ppermute | solution.py:13
  257.0 169.2 %collective-permute-start.5 = (bf16[384,2048]{1,0:T(8,128)(2,1)}, bf16[384,2048]{1,0:T(8,128)(2,1)}, u32[]{:S(2)}, u32[]{:S(2)}) collective-permute-start(bf16[384,2048]{1,0:T(8,128)(2,1)} %copy.90), channel_id=1, source_target_pairs={{8,0},{12,4},{16,8},{20,12},{24,16},{28,20},{9,1},{13,5},{17,9},{2... | collective-permute-start | bytes 4718600 | tf_op jit(solution)/shard_map/ppermute | solution.py:13
  395.2 4.2 copy-start.6
  395.3 4.2 copy-start.10
  395.3 12.5 %slice-start.3 = ((s8[4718592]{0:T(1024)(128)(4,1)}), s8[4194304]{0:T(1024)(128)(4,1)S(1)}, s32[]{:S(2)}) async-start(s8[4718592]{0:T(1024)(128)(4,1)} %bitcast.89), calls=%async_computation.8 | async-start | bytes 8388608
  399.5 8.3 %slice-start.4 = ((s8[4718592]{0:T(1024)(128)(4,1)}), s8[524288]{0:T(1024)(128)(4,1)S(1)}, s32[]{:S(2)}) async-start(s8[4718592]{0:T(1024)(128)(4,1)} %bitcast.89), calls=%async_computation.9 | async-start | bytes 1048576
  405.7 2.1 copy-start.3
  421.2 5.0 %copy-start.5 = (f32[384,2048]{1,0:T(8,128)S(1)}, f32[384,2048]{1,0:T(8,128)}, u32[]{:S(2)}) copy-start(f32[384,2048]{1,0:T(8,128)} %copy.87) | copy-start | bytes 9437188
Sparse Core Ops, SparseCore 0:
  9.5 152.3 all-gather.1
  190.6 204.6 reduce-scatter.2
  398.1 43.6 reduce-scatter.4
where the time goes:
time: 456 us; the launch traced here: 448 us
  waiting for transfers between devices  251 us (55%)
  matrix products  113 us (25%)
  local copies, waits for them, and re-layouts  34.4 us (8%)
  starting transfers between devices  20.4 us (4%)
  other arithmetic  15 us (3%)
  between operations  14.9 us (3%)
    reduce_scatter x1, waiting for transfers between devices, per_device(): lax.psum_scatter(whole_term, 'seq', scatter_dimension=1, tiled=True)  137 us
    all_gather x1, waiting for transfers between devices, per_device(): lax.all_gather(proj_weight, 'dp', axis=0, tiled=True)  62.7 us
    ppermute x8, waiting for transfers between devices, from_behind(): return lax.ppermute(block, axis, route)  38.8 us
    dot_general x3, matrix products, per_device(): jnp.einsum('hts,thd->shd', probs_b, out_heads, preferred_element_type=jnp...  26 us
    dot_general x3, matrix products, per_device(): jnp.einsum('thd,shd->hts', out_heads, value_heads, preferred_element_type...  22 us
    ppermute x8, starting transfers between devices, from_behind(): return lax.ppermute(block, axis, route)  20.1 us
    dot_general x3, matrix products, per_device(): jnp.einsum('hts,shd->thd', probs_b, value_heads, preferred_element_type=j...  17.7 us
    reduce_scatter x1, waiting for transfers between devices, per_device(): lax.psum_scatter(column_sums, 'dp', scatter_dimension=0, tiled=True)  11.7 us
  transfers between devices with their start and end apart: 11, of which 5 were waited for; matrix products, arithmetic and copies ran while one was open for 30% of the time, Pallas kernels for 0%

commit v1 on v0

v1 whole, which is shorter than its diff:
```python
import functools

import jax
import jax.numpy as jnp
from jax import lax
from jax.experimental import pallas as pl
from jax.experimental.pallas import tpu as pltpu
from jax.sharding import PartitionSpec as P

HEAD_DIM = 128
CYCLE = 2
GROUPS = 2
LOG2E = 1.4426950408889634
NEG = -1e30

NT = (((1,), (1,)), ((), ()))
NN = (((1,), (0,)), ((), ()))
TN = (((0,), (0,)), ((), ()))


def dot(a, b, dims):
    return lax.dot_general(a, b, dims, preferred_element_type=jnp.float32)


def scores_t(k, q, causal):
    s = dot(k, q, NT)
    if causal:
        key_at = lax.broadcasted_iota(jnp.int32, s.shape, 0)
        query_at = lax.broadcasted_iota(jnp.int32, s.shape, 1)
        s = jnp.where(key_at <= query_at, s, NEG)
    return s


def fwd_kernel(pos, q_ref, k0, k1, k2, v0, v1, v2, o_ref, lse_ref):
    c = HEAD_DIM ** (-0.5) * LOG2E
    q = q_ref[...]
    parts = []
    for offset, k in enumerate((k0, k1, k2)):
        parts.append(scores_t(k[...], q, offset == 0))
    tops = [jnp.max(parts[0], axis=0, keepdims=True)]
    for offset in (1, 2):
        off = jnp.where(pos[0] >= offset, 0.0, NEG)
        tops.append(jnp.max(parts[offset], axis=0, keepdims=True) + off)
    top = functools.reduce(jnp.maximum, tops) * c
    total = None
    out = None
    for offset, v in enumerate((v0, v1, v2)):
        off = jnp.where(pos[0] >= offset, 0.0, -NEG)
        e = jnp.exp2(parts[offset] * c - (top + off))
        t = jnp.sum(e, axis=0, keepdims=True)
        o = dot(v[...], e.astype(jnp.bfloat16), TN)
        total = t if total is None else total + t
        out = o if out is None else out + o
    out = out * (1.0 / total)
    o_ref[...] = out.T.astype(jnp.bfloat16)
    lse_ref[0] = top + jnp.log2(total)


def bwd_kernel(
    pos, q_ref, k0, k1, k2, v0, v1, v2, o_ref, lse_ref, do_ref,
    dq_ref, dk0, dk1, dk2, dv0, dv1, dv2,
):
    scale = HEAD_DIM ** (-0.5)
    c = scale * LOG2E
    q = q_ref[...]
    do = do_ref[...]
    prod = do.astype(jnp.float32) * o_ref[...].astype(jnp.float32)
    delta = jnp.sum(prod.T, axis=0, keepdims=True)
    lse = lse_ref[0]
    dq = None
    for offset, (k_ref, v_ref, dk, dv) in enumerate(
        ((k0, v0, dk0, dv0), (k1, v1, dk1, dv1), (k2, v2, dk2, dv2))
    ):
        k = k_ref[...]
        off = jnp.where(pos[0] >= offset, 0.0, -NEG)
        s = scores_t(k, q, offset == 0)
        p = jnp.exp2(s * c - (lse + off))
        dv[...] = dot(p.astype(jnp.bfloat16), do, NN).astype(jnp.bfloat16)
        dp = dot(v_ref[...], do, NT)
        ds = (p * (dp - delta)).astype(jnp.bfloat16)
        dk[...] = (dot(ds, q, NN) * scale).astype(jnp.bfloat16)
        part = dot(k, ds, TN)
        dq = part if dq is None else dq + part
    dq_ref[...] = (dq * scale).T.astype(jnp.bfloat16)


def head_specs(tokens, count):
    return [pl.BlockSpec((tokens, HEAD_DIM), lambda h, pos: (0, h))] * count


def lse_spec(tokens):
    return pl.BlockSpec((1, 1, tokens), lambda h, pos: (h, 0, 0))


def forward(pos, q, ks, vs):
    tokens, width = q.shape
    heads = width // HEAD_DIM
    pairs = heads * tokens * tokens * 3
    return pl.pallas_call(
        fwd_kernel,
        grid_spec=pltpu.PrefetchScalarGridSpec(
            num_scalar_prefetch=1,
            grid=(heads,),
            in_specs=head_specs(tokens, 7),
            out_specs=head_specs(tokens, 1) + [lse_spec(tokens)],
        ),
        out_shape=[
            jax.ShapeDtypeStruct((tokens, width), jnp.bfloat16),
            jax.ShapeDtypeStruct((heads, 1, tokens), jnp.float32),
        ],
        cost_estimate=pl.CostEstimate(
            flops=pairs * HEAD_DIM * 12, bytes_accessed=tokens * width * 16, transcendentals=pairs
        ),
        name="attn_fwd",
    )(pos, q, *ks, *vs)


def backward(pos, q, ks, vs, o, lse, do):
    tokens, width = q.shape
    heads = width // HEAD_DIM
    pairs = heads * tokens * tokens * 3
    return pl.pallas_call(
        bwd_kernel,
        grid_spec=pltpu.PrefetchScalarGridSpec(
            num_scalar_prefetch=1,
            grid=(heads,),
            in_specs=head_specs(tokens, 8) + [lse_spec(tokens)] + head_specs(tokens, 1),
            out_specs=head_specs(tokens, 7),
        ),
        out_shape=[jax.ShapeDtypeStruct((tokens, width), jnp.bfloat16)] * 7,
        cost_estimate=pl.CostEstimate(
            flops=pairs * HEAD_DIM * 24, bytes_accessed=tokens * width * 32, transcendentals=pairs
        ),
        name="attn_bwd",
    )(pos, q, *ks, *vs, o, lse, do)


def shifted(block, distance):
    devices = range(lax.axis_size("seq"))
    route = [(i - distance, i) for i in devices if i - distance in devices]
    return lax.ppermute(block, "seq", route)


def swapped(block):
    route = [(i, i ^ 1) for i in range(lax.axis_size("seq"))]
    return lax.ppermute(block, "seq", route)


def per_device(queries, keys, values, out_grad, proj_weight, lengths):
    f32, bf16 = jnp.float32, jnp.bfloat16
    tokens, width = queries.shape[1:]
    place = lax.axis_index("seq")
    odd = lax.rem(place, 2) == 1
    pos = place.astype(jnp.int32).reshape(1)
    query_pos = place * tokens + jnp.arange(tokens, dtype=jnp.int32)
    live = (query_pos < lengths[0]).astype(bf16)
    grad_masked = out_grad[0] * live[:, None]

    part = width // GROUPS
    groups = [slice(g * part, (g + 1) * part) for g in range(GROUPS)]
    held = []
    for g in groups:
        k0, v0 = keys[0][:, g], values[0][:, g]
        k2, v2 = shifted(k0, 2), shifted(v0, 2)
        k1 = swapped(jnp.where(odd, k2, k0))
        v1 = swapped(jnp.where(odd, v2, v0))
        held.append((queries[0][:, g], (k0, k1, k2), (v0, v1, v2)))

    half = proj_weight.shape[1] // 2
    mine = lax.rem(place, 2) * half
    w_mine = lax.all_gather(
        lax.dynamic_slice_in_dim(proj_weight, mine, half, 1), "dp", axis=0, tiled=True
    )
    w_other = swapped(w_mine)

    outs = []
    for q, ks, vs in held:
        outs.append(forward(pos, q, ks, vs))

    attn = jnp.concatenate([o for o, _ in outs], 1)
    term = dot(attn, grad_masked, TN).astype(bf16)
    column_sums = lax.psum_scatter(term, "seq", scatter_dimension=1, tiled=True)
    weight_grad = lax.psum_scatter(
        column_sums.astype(f32), "dp", scatter_dimension=0, tiled=True
    )

    grad_mine = lax.dynamic_slice_in_dim(grad_masked, mine, half, 1)
    grad_other = lax.dynamic_slice_in_dim(grad_masked, half - mine, half, 1)
    out_bwd = (dot(grad_mine, w_mine, NT) + dot(grad_other, w_other, NT)).astype(bf16)

    dqs, dks, dvs = [], [], []
    for g, (q, ks, vs), (o, lse) in zip(groups, held, outs):
        dq, dk0, dk1, dk2, dv0, dv1, dv2 = backward(pos, q, ks, vs, o, lse, out_bwd[:, g])
        dqs.append(dq)
        for into, t0, t1, t2 in ((dks, dk0, dk1, dk2), (dvs, dv0, dv1, dv2)):
            near = swapped(t1).astype(f32)
            zero = jnp.zeros_like(near)
            far = (t2.astype(f32) + jnp.where(odd, near, zero)).astype(bf16)
            far = shifted(far, -2).astype(f32)
            into.append((t0.astype(f32) + jnp.where(odd, zero, near) + far).astype(bf16))
    return (
        jnp.concatenate(dqs, 1)[None],
        jnp.concatenate(dks, 1)[None],
        jnp.concatenate(dvs, 1)[None],
        weight_grad,
    )


def solution(mesh):
    rows = P("dp", "seq", None)
    return jax.shard_map(
        per_device,
        mesh=mesh,
        in_specs=(rows, rows, rows, rows, P("dp", None), P("dp")),
        out_specs=(rows, rows, rows, P("dp", "seq")),
        check_vma=False,
    )
```

time: 456 us -> 300 us (0.66); the launches traced: 448 us -> 299 us
  matrix products: 113 us -> 16.4 us
  waiting for transfers between devices: 251 us -> 158 us
  Pallas kernels: 0 us -> 55.4 us
  local copies, waits for them, and re-layouts: 34.4 us -> 11.3 us
  starting transfers between devices: 20.4 us -> 26.4 us
    reduce_scatter x2, waiting for transfers between devices: 149 us -> 43.6 us  [the longest x1 43.6 us: per_device(): column_sums = lax.psum_scatter(term, 'seq', scatter_dimension=1, tiled=True)]
    dot_general x20 -> x3, matrix products: 113 us -> 16.4 us  [dot(): return lax.dot_general(a, b, dims, preferred_element_type=jnp.float32)]
    ppermute x8 -> x17, waiting for transfers between devices: 38.8 us -> 114 us  [the longest x8 111 us: shifted(): return lax.ppermute(block, 'seq', route)]
    all_gather x1, waiting for transfers between devices: 62.7 us -> 0.02 us  [per_device(): lax.all_gather(lax.dynamic_slice_in_dim(proj_weight, mine, half, 1), 'dp'...]
    pallas_call x0 -> x4, Pallas kernels: none -> 55.4 us  [the longest x2 32.2 us: backward(): pl.pallas_call(bwd_kernel, grid_spec=pltpu.PrefetchScalarGridSpec(num_sca...]
    reshape x5 -> x0, local copies, waits for them, and re-layouts: 13.7 us -> none  [the longest x2 5.72 us: per_device(): value_term = jnp.einsum('hts,thd->shd', probs_b, out_heads, preferred_ele...]
    convert_element_type x2 -> x0, local copies, waits for them, and re-layouts: 7.55 us -> none  [the longest x1 4.01 us: per_device(): value_accum = value_accum + value_term.astype(jnp.float32)]
    reduce_sum x1 -> x0, other arithmetic: 6.13 us -> none  [per_device(): total = total + jnp.sum(jnp.exp(scores - maximum), axis=2, keepdims=True)]
  transfers between devices with their start and end apart: 11 -> 20, of which waited for: 5 -> 10; matrix products, arithmetic and copies ran while one was open for 30% -> 12% of each run, Pallas kernels for 0% -> 19%
where the time goes in v1:
time: 300 us; the launch traced here: 299 us
  waiting for transfers between devices  158 us (53%)
  Pallas kernels  55.4 us (18%)
  starting transfers between devices  26.4 us (9%)
  between operations  16.5 us (6%)
  matrix products  16.4 us (5%)
  other arithmetic  14.5 us (5%)
  local copies, waits for them, and re-layouts  11.3 us (4%)
    ppermute x8, waiting for transfers between devices, shifted(): return lax.ppermute(block, 'seq', route)  111 us
    reduce_scatter x1, waiting for transfers between devices, per_device(): column_sums = lax.psum_scatter(term, 'seq', scatter_dimension=1, tiled=True)  43.6 us
    pallas_call x2, Pallas kernels, backward(): pl.pallas_call(bwd_kernel, grid_spec=pltpu.PrefetchScalarGridSpec(num_sca...  32.2 us
    ppermute x8, starting transfers between devices, shifted(): return lax.ppermute(block, 'seq', route)  23.8 us
    pallas_call x2, Pallas kernels, forward(): pl.pallas_call(fwd_kernel, grid_spec=pltpu.PrefetchScalarGridSpec(num_sca...  23.2 us
    dot_general x3, matrix products, dot(): return lax.dot_general(a, b, dims, preferred_element_type=jnp.float32)  16.4 us
  transfers between devices with their start and end apart: 20, of which 10 were waited for; matrix products, arithmetic and copies ran while one was open for 12% of the time, Pallas kernels for 19%

profile of v1, /device:TPU:0, one launch (start us, length us, event | category | flops | bytes accessed | tf_op | source)
XLA Modules:
  0.0 298.6 jit_solution(16167623735025549830)
XLA Ops:
  8.0 0.0 all-gather.2.cloned.1.call-start
  8.1 1.5 copy-done
  9.6 1.1 constant_dynamic-slice_fusion
  10.7 0.0 all-gather.2.cloned.1.call-update
  10.7 0.0 reduce-scatter.3.cloned.1.call-start
  10.8 1.3 slice.33.k0
  12.1 5.8 %collective-permute-start = (bf16[384,1024]{1,0:T(8,128)(2,1)S(1)}, bf16[384,1024]{1,0:T(8,128)(2,1)}, u32[]{:S(2)}, u32[]{:S(2)}) collective-permute-start(bf16[384,1024]{1,0:T(8,128)(2,1)S(1)} %slice.33.k0), channel_id=1, source_target_pairs={{0,8},{4,12},{8,16},{12,20},{16,24},{20,28},{1,9},{5,13},{9,17},{1... | collective-permute-start | bytes 2359304 | tf_op jit(solution)/shard_map/ppermute | solution.py:141
  17.9 2.1 slice.34.v0
  20.0 3.3 %collective-permute-start.2 = (bf16[384,1024]{1,0:T(8,128)(2,1)}, bf16[384,1024]{1,0:T(8,128)(2,1)}, u32[]{:S(2)}, u32[]{:S(2)}) collective-permute-start(bf16[384,1024]{1,0:T(8,128)(2,1)} %slice.34.v0), channel_id=1, source_target_pairs={{0,8},{4,12},{8,16},{12,20},{16,24},{20,28},{1,9},{5,13},{9,17},{1... | collective-permute-start | bytes 2359304 | tf_op jit(solution)/shard_map/ppermute | solution.py:141
  24.0 10.8 %collective-permute-done.k2 = bf16[384,1024]{1,0:T(8,128)(2,1)} collective-permute-done((bf16[384,1024]{1,0:T(8,128)(2,1)S(1)}, bf16[384,1024]{1,0:T(8,128)(2,1)}, u32[]{:S(2)}, u32[]{:S(2)}) %collective-permute-start) | collective-permute-done | bytes 786464 | tf_op jit(solution)/shard_map/ppermute | solution.py:141
  34.9 0.1 broadcast_select_fusion.3
  35.0 4.7 %collective-permute-start.5 = (bf16[384,1024]{1,0:T(8,128)(2,1)S(1)}, bf16[384,1024]{1,0:T(8,128)(2,1)S(1)}, u32[]{:S(2)}, u32[]{:S(2)}) collective-permute-start(bf16[384,1024]{1,0:T(8,128)(2,1)S(1)} %get-tuple-element.45.k0), channel_id=1, source_target_pairs={{0,8},{4,12},{8,16},{12,20},{16,24},{20,28},{1,9},{5,13},{9,17},{1... | collective-permute-start | bytes 2359304 | tf_op jit(solution)/shard_map/ppermute | solution.py:141
  39.7 12.1 %collective-permute-done.2.v2 = bf16[384,1024]{1,0:T(8,128)(2,1)} collective-permute-done((bf16[384,1024]{1,0:T(8,128)(2,1)}, bf16[384,1024]{1,0:T(8,128)(2,1)}, u32[]{:S(2)}, u32[]{:S(2)}) %collective-permute-start.2) | collective-permute-done | bytes 786464 | tf_op jit(solution)/shard_map/ppermute | solution.py:141
  51.8 0.1 broadcast_select_fusion.2
  52.0 4.4 %collective-permute-start.7 = (bf16[384,1024]{1,0:T(8,128)(2,1)S(1)}, bf16[384,1024]{1,0:T(8,128)(2,1)S(1)}, u32[]{:S(2)}, u32[]{:S(2)}) collective-permute-start(bf16[384,1024]{1,0:T(8,128)(2,1)S(1)} %get-tuple-element.43.v0), channel_id=1, source_target_pairs={{0,8},{4,12},{8,16},{12,20},{16,24},{20,28},{1,9},{5,13},{9,17},{1... | collective-permute-start | bytes 2359304 | tf_op jit(solution)/shard_map/ppermute | solution.py:141
  56.4 1.3 bitcast_multiply_fusion
  57.8 0.5 collective-permute-start.3
  58.3 10.3 %collective-permute-done.5.k2 = bf16[384,1024]{1,0:T(8,128)(2,1)S(1)} collective-permute-done((bf16[384,1024]{1,0:T(8,128)(2,1)S(1)}, bf16[384,1024]{1,0:T(8,128)(2,1)S(1)}, u32[]{:S(2)}, u32[]{:S(2)}) %collective-permute-start.5) | collective-permute-done | bytes 786464 | tf_op jit(solution)/shard_map/ppermute | solution.py:141
  68.6 1.1 broadcast_select_fusion.1
  69.7 14.6 %collective-permute-done.7.v2 = bf16[384,1024]{1,0:T(8,128)(2,1)S(1)} collective-permute-done((bf16[384,1024]{1,0:T(8,128)(2,1)S(1)}, bf16[384,1024]{1,0:T(8,128)(2,1)S(1)}, u32[]{:S(2)}, u32[]{:S(2)}) %collective-permute-start.7) | collective-permute-done | bytes 786464 | tf_op jit(solution)/shard_map/ppermute | solution.py:141
  84.3 1.1 broadcast_select_fusion
  85.4 1.3 fusion.31
  86.7 0.8 copy-done.22
  87.5 0.9 copy-done.23
  88.4 11.5 %attn_fwd.2 = (bf16[384,1024]{1,0:T(8,128)(2,1)}, f32[8,1,384]{2,1,0:T(1,128)}) custom-call(s32[1]{0:T(128)} %bitcast.pos, bf16[384,1024]{1,0:T(8,128)(2,1)} %get-tuple-element.46.q_ref, bf16[384,1024]{1,0:T(8,128)(2,1)} %copy-done.13, bf16[384,1024]{1,0:T(8,128)(2,1)} %copy-done.22, bf16[384,1024]{1,0:T(8,128)(2,1)} %collective-permute-done.k2, ...), custom_call_target="tpu_custom_call" | custom-call | flops 5435817984 | bytes 6291456 | tf_op jit(solution)/shard_map/attn_fwd/pallas_call | solution.py:99
  100.0 0.9 copy-done.21
  100.9 11.7 %attn_fwd.3 = (bf16[384,1024]{1,0:T(8,128)(2,1)}, f32[8,1,384]{2,1,0:T(1,128)}) custom-call(s32[1]{0:T(128)} %bitcast.pos, bf16[384,1024]{1,0:T(8,128)(2,1)} %get-tuple-element.47.q_ref, bf16[384,1024]{1,0:T(8,128)(2,1)} %copy-done.14, bf16[384,1024]{1,0:T(8,128)(2,1)} %copy-done.21, bf16[384,1024]{1,0:T(8,128)(2,1)} %copy-done.7, ...), custom_call_target="tpu_custom_call" | custom-call | flops 5435817984 | bytes 6291456 | tf_op jit(solution)/shard_map/attn_fwd/pallas_call | solution.py:99
  112.6 8.3 %convolution_convert_fusion = bf16[2048,2048]{1,0:T(8,128)(2,1)} fusion(bf16[384,2048]{1,0:T(8,128)(2,1)S(1)} %copy-done.6, bf16[384,1024]{1,0:T(8,128)(2,1)} %get-tuple-element.25.o_ref, bf16[384,1024]{1,0:T(8,128)(2,1)} %get-tuple-element.22.o_ref), kind=kOutput, calls=%fused_computation | convolution fusion | flops 3228565504 | bytes 11534336 | tf_op jit(solution)/shard_map/dot_general | solution.py:22
  120.8 0.0 reduce-scatter.3.cloned.1.call-update
  120.8 0.2 reduce-scatter.5.cloned.1.call-start
  121.1 0.0 all-gather.2.cloned.1.call-done
  121.1 0.6 collective-permute-start.4
  121.7 4.0 %fusion.24 = f32[384,2048]{1,0:T(8,128)S(1)} fusion(bf16[2048,1024]{1,0:T(8,128)(2,1)} %all-gather.2.cloned.1.call-done, bf16[384,2048]{1,0:T(8,128)(2,1)S(1)} %copy-done.6, s32[]{:T(128)S(6)} %select_n.64), kind=kOutput, calls=%fused_computation.38 | convolution fusion | flops 1610612736 | bytes 8126468 | tf_op jit(solution)/shard_map/dot_general | solution.py:22
  125.7 3.2 %collective-permute-done.4 = bf16[2048,1024]{1,0:T(8,128)(2,1)} collective-permute-done((bf16[2048,1024]{1,0:T(8,128)(2,1)}, bf16[2048,1024]{1,0:T(8,128)(2,1)}, u32[]{:S(2)}, u32[]{:S(2)}) %collective-permute-start.4) | collective-permute-done | bytes 4194336 | tf_op jit(solution)/shard_map/ppermute | solution.py:146
  128.8 4.2 %add_convert_fusion = bf16[384,2048]{1,0:T(8,128)(2,1)S(1)} fusion(f32[384,2048]{1,0:T(8,128)S(1)} %fusion.24, bf16[2048,1024]{1,0:T(8,128)(2,1)} %collective-permute-done.4, bf16[384,2048]{1,0:T(8,128)(2,1)S(1)} %copy-done.6, s32[]{:T(128)S(6)} %select_n.65), kind=kOutput, calls=%fused_computation.1 | convolution fusion | flops 1612185600 | bytes 9699332 | tf_op jit(solution)/shard_map/dot_general | solution.py:22
  133.0 1.3 fusion.30
  134.3 16.2 %attn_bwd.2 = (bf16[384,1024]{1,0:T(8,128)(2,1)}, bf16[384,1024]{1,0:T(8,128)(2,1)}, bf16[384,1024]{1,0:T(8,128)(2,1)}, bf16[384,1024]{1,0:T(8,128)(2,1)}, bf16[...) custom-call(s32[1]{0:T(128)} %bitcast.pos, bf16[384,1024]{1,0:T(8,128)(2,1)} %get-tuple-element.46.q_ref, ...), custom_call_target="tpu_custom_call" | custom-call | flops 10871635968 | bytes 12582912 | tf_op jit(solution)/shard_map/attn_bwd/pallas_call | solution.py:122
  150.5 0.6 collective-permute-start.13
  151.0 43.6 %reduce-scatter.3.cloned.1.call-done = bf16[2048,256]{1,0:T(8,128)(2,1)} async-done(((bf16[2048,2048]{1,0:T(8,128)(2,1)}), bf16[2048,256]{1,0:T(8,128)(2,1)}) %reduce-scatter.3.cloned.1.call-update) | async-done | bytes 1048592 | tf_op jit(solution)/shard_map/reduce_scatter | solution.py:182
  194.6 2.7 convert_element_type.115
  197.4 0.0 reduce-scatter.5.cloned.1.call-update
  197.4 16.0 %attn_bwd.3 = (bf16[384,1024]{1,0:T(8,128)(2,1)}, bf16[384,1024]{1,0:T(8,128)(2,1)}, bf16[384,1024]{1,0:T(8,128)(2,1)}, bf16[384,1024]{1,0:T(8,128)(2,1)}, bf16[...) custom-call(s32[1]{0:T(128)} %bitcast.pos, bf16[384,1024]{1,0:T(8,128)(2,1)} %get-tuple-element.47.q_ref, ...), custom_call_target="tpu_custom_call" | custom-call | flops 10871635968 | bytes 12582912 | tf_op jit(solution)/shard_map/attn_bwd/pallas_call | solution.py:122
  213.4 0.1 collective-permute-start.15
  213.5 0.5 collective-permute-start.9
  214.0 0.1 collective-permute-start.11
  214.1 2.5 maximum_bitcast_fusion
  216.6 0.3 fusion.14
  216.9 1.4 collective-permute-start.14
  218.4 0.3 fusion.19
  218.7 1.4 collective-permute-start.16
  220.1 0.3 fusion.4
  220.4 1.4 collective-permute-start.10
  221.9 0.3 fusion.9
  222.2 1.3 collective-permute-start.12
  223.5 15.9 %collective-permute-done.14 = bf16[384,1024]{1,0:T(8,128)(2,1)S(1)} collective-permute-done((bf16[384,1024]{1,0:T(8,128)(2,1)S(1)}, bf16[384,1024]{1,0:T(8,128)(2,1)S(1)}, u32[]{:S(2)}, u32[]{:S(2)}) %collective-permute-start.14) | collective-permute-done | bytes 786464 | tf_op jit(solution)/shard_map/ppermute | solution.py:141
  239.4 0.5 fusion.12
  239.8 16.4 %collective-permute-done.16 = bf16[384,1024]{1,0:T(8,128)(2,1)S(1)} collective-permute-done((bf16[384,1024]{1,0:T(8,128)(2,1)S(1)}, bf16[384,1024]{1,0:T(8,128)(2,1)S(1)}, u32[]{:S(2)}, u32[]{:S(2)}) %collective-permute-start.16) | collective-permute-done | bytes 786464 | tf_op jit(solution)/shard_map/ppermute | solution.py:141
  256.2 0.5 fusion.17
  256.7 1.3 maximum_bitcast_fusion.2
  258.0 15.1 %collective-permute-done.10 = bf16[384,1024]{1,0:T(8,128)(2,1)S(1)} collective-permute-done((bf16[384,1024]{1,0:T(8,128)(2,1)S(1)}, bf16[384,1024]{1,0:T(8,128)(2,1)S(1)}, u32[]{:S(2)}, u32[]{:S(2)}) %collective-permute-start.10) | collective-permute-done | bytes 786464 | tf_op jit(solution)/shard_map/ppermute | solution.py:141
  273.1 0.5 fusion.2
  273.5 15.9 %collective-permute-done.12 = bf16[384,1024]{1,0:T(8,128)(2,1)S(1)} collective-permute-done((bf16[384,1024]{1,0:T(8,128)(2,1)S(1)}, bf16[384,1024]{1,0:T(8,128)(2,1)S(1)}, u32[]{:S(2)}, u32[]{:S(2)}) %collective-permute-start.12) | collective-permute-done | bytes 786464 | tf_op jit(solution)/shard_map/ppermute | solution.py:141
  289.4 0.5 fusion.7
  289.9 1.2 maximum_bitcast_fusion.1
  (57 shorter events, 0.1 us)
Async XLA Ops:
  8.0 1.6 copy-start
  8.0 113.1 %all-gather.2.cloned.1.call-start = ((), (), s32[]{:S(2)}) async-start(), calls=%async_computation.2 | async-start | bytes 5242880 | tf_op jit(solution)/shard_map/all_gather | solution.py:171
  10.7 183.9 %reduce-scatter.3.cloned.1.call-start = ((), (), s32[]{:S(2)}) async-start(), calls=%async_computation.3 | async-start | bytes 9437184 | tf_op jit(solution)/shard_map/reduce_scatter | solution.py:182
  10.7 24.1 %copy-start.2 = (bf16[1,384,2048]{2,1,0:T(8,128)(2,1)S(1)}, bf16[1,384,2048]{2,1,0:T(8,128)(2,1)}, u32[]{:S(2)}) copy-start(bf16[1,384,2048]{2,1,0:T(8,128)(2,1)} %param.7) | copy-start | bytes 4718596
  12.1 23.0 %copy-start.13 = (bf16[384,1024]{1,0:T(8,128)(2,1)}, bf16[384,1024]{1,0:T(8,128)(2,1)S(1)}, u32[]{:S(2)}) copy-start(bf16[384,1024]{1,0:T(8,128)(2,1)S(1)} %slice.33.k0) | copy-start | bytes 2359300
  12.1 22.8 %collective-permute-start = (bf16[384,1024]{1,0:T(8,128)(2,1)S(1)}, bf16[384,1024]{1,0:T(8,128)(2,1)}, u32[]{:S(2)}, u32[]{:S(2)}) collective-permute-start(bf16[384,1024]{1,0:T(8,128)(2,1)S(1)} %slice.33.k0), channel_id=1, source_target_pairs={{0,8},{4,12},{8,16},{12,20},{16,24},{20,28},{1,9},{5,13},{9,17},{1... | collective-permute-start | bytes 2359304 | tf_op jit(solution)/shard_map/ppermute | solution.py:141
  20.0 31.8 %collective-permute-start.2 = (bf16[384,1024]{1,0:T(8,128)(2,1)}, bf16[384,1024]{1,0:T(8,128)(2,1)}, u32[]{:S(2)}, u32[]{:S(2)}) collective-permute-start(bf16[384,1024]{1,0:T(8,128)(2,1)} %slice.34.v0), channel_id=1, source_target_pairs={{0,8},{4,12},{8,16},{12,20},{16,24},{20,28},{1,9},{5,13},{9,17},{1... | collective-permute-start | bytes 2359304 | tf_op jit(solution)/shard_map/ppermute | solution.py:141
  24.0 27.8 %copy-start.3 = (bf16[1,384,2048]{2,1,0:T(8,128)(2,1)S(1)}, bf16[1,384,2048]{2,1,0:T(8,128)(2,1)}, u32[]{:S(2)}) copy-start(bf16[1,384,2048]{2,1,0:T(8,128)(2,1)} %param.8) | copy-start | bytes 4718596
  35.0 17.0 %copy-start.14 = (bf16[384,1024]{1,0:T(8,128)(2,1)}, bf16[384,1024]{1,0:T(8,128)(2,1)S(1)}, u32[]{:S(2)}) copy-start(bf16[384,1024]{1,0:T(8,128)(2,1)S(1)} %get-tuple-element.45.k0) | copy-start | bytes 2359300
  35.0 21.4 %copy-start.4 = (bf16[1,384,2048]{2,1,0:T(8,128)(2,1)S(1)}, bf16[1,384,2048]{2,1,0:T(8,128)(2,1)}, u32[]{:S(2)}) copy-start(bf16[1,384,2048]{2,1,0:T(8,128)(2,1)} %param.9) | copy-start | bytes 4718596
  35.0 33.5 %collective-permute-start.5 = (bf16[384,1024]{1,0:T(8,128)(2,1)S(1)}, bf16[384,1024]{1,0:T(8,128)(2,1)S(1)}, u32[]{:S(2)}, u32[]{:S(2)}) collective-permute-start(bf16[384,1024]{1,0:T(8,128)(2,1)S(1)} %get-tuple-element.45.k0), channel_id=1, source_target_pairs={{0,8},{4,12},{8,16},{12,20},{16,24},{20,28},{1,9},{5,13},{9,17},{1... | collective-permute-start | bytes 2359304 | tf_op jit(solution)/shard_map/ppermute | solution.py:141
  52.0 5.8 %copy-start.15 = (bf16[384,1024]{1,0:T(8,128)(2,1)}, bf16[384,1024]{1,0:T(8,128)(2,1)S(1)}, u32[]{:S(2)}) copy-start(bf16[384,1024]{1,0:T(8,128)(2,1)S(1)} %get-tuple-element.43.v0) | copy-start | bytes 2359300
  52.0 32.3 %collective-permute-start.7 = (bf16[384,1024]{1,0:T(8,128)(2,1)S(1)}, bf16[384,1024]{1,0:T(8,128)(2,1)S(1)}, u32[]{:S(2)}, u32[]{:S(2)}) collective-permute-start(bf16[384,1024]{1,0:T(8,128)(2,1)S(1)} %get-tuple-element.43.v0), channel_id=1, source_target_pairs={{0,8},{4,12},{8,16},{12,20},{16,24},{20,28},{1,9},{5,13},{9,17},{1... | collective-permute-start | bytes 2359304 | tf_op jit(solution)/shard_map/ppermute | solution.py:141
  57.8 28.9 %collective-permute-start.1 = (bf16[384,1024]{1,0:T(8,128)(2,1)S(1)}, bf16[384,1024]{1,0:T(8,128)(2,1)S(1)}, u32[]{:S(2)}, u32[]{:S(2)}) collective-permute-start(bf16[384,1024]{1,0:T(8,128)(2,1)S(1)} %get-tuple-element.44), channel_id=1, source_target_pairs={{0,4},{4,0},{8,12},{12,8},{16,20},{20,16},{24,28},{28,24},{1,5},{5... | collective-permute-start | bytes 2359304 | tf_op jit(solution)/shard_map/ppermute | solution.py:146
  57.8 28.9 %collective-permute-start.3 = (bf16[384,1024]{1,0:T(8,128)(2,1)S(1)}, bf16[384,1024]{1,0:T(8,128)(2,1)S(1)}, u32[]{:S(2)}, u32[]{:S(2)}) collective-permute-start(bf16[384,1024]{1,0:T(8,128)(2,1)S(1)} %get-tuple-element.42), channel_id=1, source_target_pairs={{0,4},{4,0},{8,12},{12,8},{16,20},{20,16},{24,28},{28,24},{1,5},{5... | collective-permute-start | bytes 2359304 | tf_op jit(solution)/shard_map/ppermute | solution.py:146
  68.6 16.8 %copy-start.7 = (bf16[384,1024]{1,0:T(8,128)(2,1)}, bf16[384,1024]{1,0:T(8,128)(2,1)S(1)}, u32[]{:S(2)}) copy-start(bf16[384,1024]{1,0:T(8,128)(2,1)S(1)} %collective-permute-done.5.k2) | copy-start | bytes 2359300
  69.7 15.7 %copy-start.5 = (bf16[1,384,2048]{2,1,0:T(8,128)(2,1)S(1)}, bf16[1,384,2048]{2,1,0:T(8,128)(2,1)}, u32[]{:S(2)}) copy-start(bf16[1,384,2048]{2,1,0:T(8,128)(2,1)} %param.6) | copy-start | bytes 4718596
  69.7 30.3 %collective-permute-start.6 = (bf16[384,1024]{1,0:T(8,128)(2,1)}, bf16[384,1024]{1,0:T(8,128)(2,1)S(1)}, u32[]{:S(2)}, u32[]{:S(2)}) collective-permute-start(bf16[384,1024]{1,0:T(8,128)(2,1)} %broadcast_select_fusion.1), channel_id=1, source_target_pairs={{0,4},{4,0},{8,12},{12,8},{16,20},{20,16},{24,28},{28,24},{1,5},{5... | collective-permute-start | bytes 2359304 | tf_op jit(solution)/shard_map/ppermute | solution.py:146
  84.3 2.4 copy-start.8
  85.4 14.6 %collective-permute-start.8 = (bf16[384,1024]{1,0:T(8,128)(2,1)}, bf16[384,1024]{1,0:T(8,128)(2,1)}, u32[]{:S(2)}, u32[]{:S(2)}) collective-permute-start(bf16[384,1024]{1,0:T(8,128)(2,1)} %broadcast_select_fusion), channel_id=1, source_target_pairs={{0,4},{4,0},{8,12},{12,8},{16,20},{20,16},{24,28},{28,24},{1,5},{5... | collective-permute-start | bytes 2359304 | tf_op jit(solution)/shard_map/ppermute | solution.py:146
  86.7 0.9 copy-start.22
  87.5 0.9 copy-start.23
  100.0 0.9 copy-start.21
  100.9 11.7 %copy-start.6 = (bf16[384,2048]{1,0:T(8,128)(2,1)S(1)}, bf16[384,2048]{1,0:T(8,128)(2,1)}, u32[]{:S(2)}) copy-start(bf16[384,2048]{1,0:T(8,128)(2,1)} %bitcast_multiply_fusion) | copy-start | bytes 4718596
  120.8 170.3 %reduce-scatter.5.cloned.1.call-start = ((), (), s32[]{:S(2)}) async-start(), calls=%async_computation.4 | async-start | bytes 2621440 | tf_op jit(solution)/shard_map/reduce_scatter | solution.py:183
  121.1 7.7 %collective-permute-start.4 = (bf16[2048,1024]{1,0:T(8,128)(2,1)}, bf16[2048,1024]{1,0:T(8,128)(2,1)}, u32[]{:S(2)}, u32[]{:S(2)}) collective-permute-start(bf16[2048,1024]{1,0:T(8,128)(2,1)} %all-gather.2.cloned.1.call-done), channel_id=1, source_target_pairs={{0,4},{4,0},{8,12},{12,8},{16,20},{20,16},{24,28},{28,24},{1,5},{5... | collective-permute-start | bytes 12582920 | tf_op jit(solution)/shard_map/ppermute | solution.py:146
  150.5 66.1 %collective-permute-start.13 = (bf16[384,1024]{1,0:T(8,128)(2,1)}, bf16[384,1024]{1,0:T(8,128)(2,1)S(1)}, u32[]{:S(2)}, u32[]{:S(2)}) collective-permute-start(bf16[384,1024]{1,0:T(8,128)(2,1)} %get-tuple-element.35), channel_id=1, source_target_pairs={{0,4},{4,0},{8,12},{12,8},{16,20},{20,16},{24,28},{28,24},{1,5},{5... | collective-permute-start | bytes 2359304 | tf_op jit(solution)/shard_map/ppermute | solution.py:146
  197.4 16.7 %copy-start.16 = (bf16[384,1024]{1,0:T(8,128)(2,1)S(1)}, bf16[384,1024]{1,0:T(8,128)(2,1)}, u32[]{:S(2)}) copy-start(bf16[384,1024]{1,0:T(8,128)(2,1)} %get-tuple-element.24) | copy-start | bytes 2359300
  213.4 4.9 %collective-permute-start.15 = (bf16[384,1024]{1,0:T(8,128)(2,1)}, bf16[384,1024]{1,0:T(8,128)(2,1)S(1)}, u32[]{:S(2)}, u32[]{:S(2)}) collective-permute-start(bf16[384,1024]{1,0:T(8,128)(2,1)} %get-tuple-element.38), channel_id=1, source_target_pairs={{0,4},{4,0},{8,12},{12,8},{16,20},{20,16},{24,28},{28,24},{1,5},{5... | collective-permute-start | bytes 2359304 | tf_op jit(solution)/shard_map/ppermute | solution.py:146
  213.5 6.6 %collective-permute-start.9 = (bf16[384,1024]{1,0:T(8,128)(2,1)}, bf16[384,1024]{1,0:T(8,128)(2,1)S(1)}, u32[]{:S(2)}, u32[]{:S(2)}) collective-permute-start(bf16[384,1024]{1,0:T(8,128)(2,1)} %get-tuple-element.29), channel_id=1, source_target_pairs={{0,4},{4,0},{8,12},{12,8},{16,20},{20,16},{24,28},{28,24},{1,5},{5... | collective-permute-start | bytes 2359304 | tf_op jit(solution)/shard_map/ppermute | solution.py:146
  214.0 7.9 %collective-permute-start.11 = (bf16[384,1024]{1,0:T(8,128)(2,1)}, bf16[384,1024]{1,0:T(8,128)(2,1)S(1)}, u32[]{:S(2)}, u32[]{:S(2)}) collective-permute-start(bf16[384,1024]{1,0:T(8,128)(2,1)} %get-tuple-element.32), channel_id=1, source_target_pairs={{0,4},{4,0},{8,12},{12,8},{16,20},{20,16},{24,28},{28,24},{1,5},{5... | collective-permute-start | bytes 2359304 | tf_op jit(solution)/shard_map/ppermute | solution.py:146
  214.1 2.5 copy-start.10
  216.6 1.8 copy-start.12
  216.9 3.2 %copy-start.9 = (bf16[384,1024]{1,0:T(8,128)(2,1)S(1)}, bf16[384,1024]{1,0:T(8,128)(2,1)}, u32[]{:S(2)}) copy-start(bf16[384,1024]{1,0:T(8,128)(2,1)} %get-tuple-element.30) | copy-start | bytes 2359300
  216.9 22.4 %collective-permute-start.14 = (bf16[384,1024]{1,0:T(8,128)(2,1)S(1)}, bf16[384,1024]{1,0:T(8,128)(2,1)S(1)}, u32[]{:S(2)}, u32[]{:S(2)}) collective-permute-start(bf16[384,1024]{1,0:T(8,128)(2,1)S(1)} %fusion.14), channel_id=1, source_target_pairs={{8,0},{12,4},{16,8},{20,12},{24,16},{28,20},{9,1},{13,5},{17,9},{2... | collective-permute-start | bytes 2359304 | tf_op jit(solution)/shard_map/ppermute | solution.py:141
  218.7 3.2 %copy-start.11 = (bf16[384,1024]{1,0:T(8,128)(2,1)S(1)}, bf16[384,1024]{1,0:T(8,128)(2,1)}, u32[]{:S(2)}) copy-start(bf16[384,1024]{1,0:T(8,128)(2,1)} %get-tuple-element.33) | copy-start | bytes 2359300
  218.7 37.5 %collective-permute-start.16 = (bf16[384,1024]{1,0:T(8,128)(2,1)S(1)}, bf16[384,1024]{1,0:T(8,128)(2,1)S(1)}, u32[]{:S(2)}, u32[]{:S(2)}) collective-permute-start(bf16[384,1024]{1,0:T(8,128)(2,1)S(1)} %fusion.19), channel_id=1, source_target_pairs={{8,0},{12,4},{16,8},{20,12},{24,16},{28,20},{9,1},{13,5},{17,9},{2... | collective-permute-start | bytes 2359304 | tf_op jit(solution)/shard_map/ppermute | solution.py:141
  220.4 18.9 %copy-start.18 = (bf16[384,1024]{1,0:T(8,128)(2,1)S(1)}, bf16[384,1024]{1,0:T(8,128)(2,1)}, u32[]{:S(2)}) copy-start(bf16[384,1024]{1,0:T(8,128)(2,1)} %get-tuple-element.34) | copy-start | bytes 2359300
  220.4 52.6 %collective-permute-start.10 = (bf16[384,1024]{1,0:T(8,128)(2,1)S(1)}, bf16[384,1024]{1,0:T(8,128)(2,1)S(1)}, u32[]{:S(2)}, u32[]{:S(2)}) collective-permute-start(bf16[384,1024]{1,0:T(8,128)(2,1)S(1)} %fusion.4), channel_id=1, source_target_pairs={{8,0},{12,4},{16,8},{20,12},{24,16},{28,20},{9,1},{13,5},{17,9},{2... | collective-permute-start | bytes 2359304 | tf_op jit(solution)/shard_map/ppermute | solution.py:141
  222.2 67.2 %collective-permute-start.12 = (bf16[384,1024]{1,0:T(8,128)(2,1)S(1)}, bf16[384,1024]{1,0:T(8,128)(2,1)S(1)}, u32[]{:S(2)}, u32[]{:S(2)}) collective-permute-start(bf16[384,1024]{1,0:T(8,128)(2,1)S(1)} %fusion.9), channel_id=1, source_target_pairs={{8,0},{12,4},{16,8},{20,12},{24,16},{28,20},{9,1},{13,5},{17,9},{2... | collective-permute-start | bytes 2359304 | tf_op jit(solution)/shard_map/ppermute | solution.py:141
  239.4 16.9 %copy-start.20 = (bf16[384,1024]{1,0:T(8,128)(2,1)S(1)}, bf16[384,1024]{1,0:T(8,128)(2,1)}, u32[]{:S(2)}) copy-start(bf16[384,1024]{1,0:T(8,128)(2,1)} %get-tuple-element.37) | copy-start | bytes 2359300
  256.7 16.4 %copy-start.17 = (bf16[384,1024]{1,0:T(8,128)(2,1)S(1)}, bf16[384,1024]{1,0:T(8,128)(2,1)}, u32[]{:S(2)}) copy-start(bf16[384,1024]{1,0:T(8,128)(2,1)} %get-tuple-element.28) | copy-start | bytes 2359300
  273.1 16.3 %copy-start.19 = (bf16[384,1024]{1,0:T(8,128)(2,1)S(1)}, bf16[384,1024]{1,0:T(8,128)(2,1)}, u32[]{:S(2)}) copy-start(bf16[384,1024]{1,0:T(8,128)(2,1)} %get-tuple-element.31) | copy-start | bytes 2359300
  289.4 1.7 copy-start.1
Sparse Core Ops, SparseCore 0:
  11.0 83.5 all-gather.1
  197.5 43.6 reduce-scatter.4
Sparse Core Ops, SparseCore 1:
  120.9 73.6 reduce-scatter.2

commit v2 on v1

--- a/solution.py
+++ b/solution.py
@@ -7,8 +7,8 @@
 from jax.experimental.pallas import tpu as pltpu
 from jax.sharding import PartitionSpec as P
 
+
 HEAD_DIM = 128
-CYCLE = 2
 GROUPS = 2
 LOG2E = 1.4426950408889634
 NEG = -1e30
@@ -58,7 +58,7 @@
 
 def bwd_kernel(
     pos, q_ref, k0, k1, k2, v0, v1, v2, o_ref, lse_ref, do_ref,
-    dq_ref, dk0, dk1, dk2, dv0, dv1, dv2,
+    dq_ref, t0, t1, t2,
 ):
     scale = HEAD_DIM ** (-0.5)
     c = scale * LOG2E
@@ -68,17 +68,15 @@
     delta = jnp.sum(prod.T, axis=0, keepdims=True)
     lse = lse_ref[0]
     dq = None
-    for offset, (k_ref, v_ref, dk, dv) in enumerate(
-        ((k0, v0, dk0, dv0), (k1, v1, dk1, dv1), (k2, v2, dk2, dv2))
-    ):
+    for offset, (k_ref, v_ref, term) in enumerate(((k0, v0, t0), (k1, v1, t1), (k2, v2, t2))):
         k = k_ref[...]
         off = jnp.where(pos[0] >= offset, 0.0, -NEG)
         s = scores_t(k, q, offset == 0)
         p = jnp.exp2(s * c - (lse + off))
-        dv[...] = dot(p.astype(jnp.bfloat16), do, NN).astype(jnp.bfloat16)
+        term[1] = dot(p.astype(jnp.bfloat16), do, NN).astype(jnp.bfloat16)
         dp = dot(v_ref[...], do, NT)
         ds = (p * (dp - delta)).astype(jnp.bfloat16)
-        dk[...] = (dot(ds, q, NN) * scale).astype(jnp.bfloat16)
+        term[0] = (dot(ds, q, NN) * scale).astype(jnp.bfloat16)
         part = dot(k, ds, TN)
         dq = part if dq is None else dq + part
     dq_ref[...] = (dq * scale).T.astype(jnp.bfloat16)
@@ -125,9 +123,11 @@
             num_scalar_prefetch=1,
             grid=(heads,),
             in_specs=head_specs(tokens, 8) + [lse_spec(tokens)] + head_specs(tokens, 1),
-            out_specs=head_specs(tokens, 7),
-        ),
-        out_shape=[jax.ShapeDtypeStruct((tokens, width), jnp.bfloat16)] * 7,
+            out_specs=head_specs(tokens, 1)
+            + [pl.BlockSpec((2, tokens, HEAD_DIM), lambda h, pos: (0, 0, h))] * 3,
+        ),
+        out_shape=[jax.ShapeDtypeStruct((tokens, width), jnp.bfloat16)]
+        + [jax.ShapeDtypeStruct((2, tokens, width), jnp.bfloat16)] * 3,
         cost_estimate=pl.CostEstimate(
             flops=pairs * HEAD_DIM * 24, bytes_accessed=tokens * width * 32, transcendentals=pairs
         ),
@@ -141,12 +141,21 @@
     return lax.ppermute(block, "seq", route)
 
 
+def ring_to(block, axis, distance):
+    count = lax.axis_size(axis)
+    return lax.ppermute(block, axis, [(i, (i + distance) % count) for i in range(count)])
+
+
 def swapped(block):
     route = [(i, i ^ 1) for i in range(lax.axis_size("seq"))]
     return lax.ppermute(block, "seq", route)
 
 
-def per_device(queries, keys, values, out_grad, proj_weight, lengths):
+def after(arrays, *earlier):
+    return lax.optimization_barrier((*arrays, *earlier))[: len(arrays)]
+
+
+def layer(queries, keys, values, out_grad, proj_weight, lengths):
     f32, bf16 = jnp.float32, jnp.bfloat16
     tokens, width = queries.shape[1:]
     place = lax.axis_index("seq")
@@ -158,50 +167,87 @@
 
     part = width // GROUPS
     groups = [slice(g * part, (g + 1) * part) for g in range(GROUPS)]
-    held = []
-    for g in groups:
-        k0, v0 = keys[0][:, g], values[0][:, g]
-        k2, v2 = shifted(k0, 2), shifted(v0, 2)
-        k1 = swapped(jnp.where(odd, k2, k0))
-        v1 = swapped(jnp.where(odd, v2, v0))
-        held.append((queries[0][:, g], (k0, k1, k2), (v0, v1, v2)))
+    near = [(queries[0][:, g], keys[0][:, g], values[0][:, g]) for g in groups]
+    far = []
+    for _, k0, v0 in near:
+        k2 = shifted(k0, 2)
+        far.append((k2, shifted(v0, 2)))
 
     half = proj_weight.shape[1] // 2
-    mine = lax.rem(place, 2) * half
+    parity = lax.rem(place, 2)
+    mine = parity * half
     w_mine = lax.all_gather(
         lax.dynamic_slice_in_dim(proj_weight, mine, half, 1), "dp", axis=0, tiled=True
     )
     w_other = swapped(w_mine)
 
-    outs = []
-    for q, ks, vs in held:
-        outs.append(forward(pos, q, ks, vs))
+    held, outs = [], []
+    for (q, k0, v0), (k2, v2) in zip(near, far):
+        if outs:
+            k2, v2 = after((k2, v2), outs[-1][0])
+        k1 = swapped(jnp.where(odd, k2, k0))
+        v1 = swapped(jnp.where(odd, v2, v0))
+        held.append((q, (k0, k1, k2), (v0, v1, v2)))
+        outs.append(forward(pos, *held[-1]))
 
     attn = jnp.concatenate([o for o, _ in outs], 1)
-    term = dot(attn, grad_masked, TN).astype(bf16)
-    column_sums = lax.psum_scatter(term, "seq", scatter_dimension=1, tiled=True)
-    weight_grad = lax.psum_scatter(
-        column_sums.astype(f32), "dp", scatter_dimension=0, tiled=True
-    )
+    attn_pair = jnp.concatenate([attn, swapped(attn)], 0)
+    chips = lax.axis_size("seq") // 2
+    chip = place // 2
+    own = grad_masked.shape[1] // (2 * chips)
+    by_owner = grad_masked.reshape(tokens, chips, 2, own)
+
+    def owned_by(core):
+        return lax.dynamic_index_in_dim(by_owner, core, 2, False).reshape(tokens, chips * own)
+
+    grad_pair = jnp.concatenate([owned_by(parity), swapped(owned_by(1 - parity))], 0)
+    pieces = []
+    for step in list(range(1, chips)) + [0]:
+        at = lax.rem(chip + step, chips) * own
+        piece = dot(attn_pair, lax.dynamic_slice_in_dim(grad_pair, at, own, 1), TN)
+        pieces.append(piece.astype(bf16) if step else piece)
+    arrived = []
+    for step, piece in enumerate(pieces[:-1], 1):
+        arrived.append(ring_to(piece, "seq", 2 * step))
 
     grad_mine = lax.dynamic_slice_in_dim(grad_masked, mine, half, 1)
     grad_other = lax.dynamic_slice_in_dim(grad_masked, half - mine, half, 1)
+    (grad_mine,) = after((grad_mine,), *pieces)
     out_bwd = (dot(grad_mine, w_mine, NT) + dot(grad_other, w_other, NT)).astype(bf16)
 
-    dqs, dks, dvs = [], [], []
+    dqs, terms, sends = [], [], []
     for g, (q, ks, vs), (o, lse) in zip(groups, held, outs):
-        dq, dk0, dk1, dk2, dv0, dv1, dv2 = backward(pos, q, ks, vs, o, lse, out_bwd[:, g])
+        do = out_bwd[:, g]
+        if sends:
+            (do,) = after((do,), sends[-1])
+        dq, t0, t1, t2 = backward(pos, q, ks, vs, o, lse, do)
         dqs.append(dq)
-        for into, t0, t1, t2 in ((dks, dk0, dk1, dk2), (dvs, dv0, dv1, dv2)):
-            near = swapped(t1).astype(f32)
-            zero = jnp.zeros_like(near)
-            far = (t2.astype(f32) + jnp.where(odd, near, zero)).astype(bf16)
-            far = shifted(far, -2).astype(f32)
-            into.append((t0.astype(f32) + jnp.where(odd, zero, near) + far).astype(bf16))
+        beside = swapped(t1).astype(f32)
+        zero = jnp.zeros_like(beside)
+        sends.append((t2.astype(f32) + jnp.where(odd, beside, zero)).astype(bf16))
+        terms.append(t0.astype(f32) + jnp.where(odd, zero, beside))
+    behind = []
+    for send in sends:
+        behind.append(shifted(send, -2))
+
+    arrived = after(tuple(arrived), dqs[-1])
+    sums = pieces[-1]
+    for piece in arrived:
+        sums = sums + piece.astype(f32)
+    rows = proj_weight.shape[0]
+    here = lax.axis_index("dp")
+    count = lax.axis_size("dp")
+    weight_grad = lax.dynamic_slice_in_dim(sums, here * rows, rows, 0)
+    for step in range(1, count):
+        at = lax.rem(here + step, count) * rows
+        piece = lax.dynamic_slice_in_dim(sums, at, rows, 0).astype(bf16)
+        weight_grad = weight_grad + ring_to(piece, "dp", step).astype(f32)
+
+    totals = [(t + b.astype(f32)).astype(bf16) for t, b in zip(terms, behind)]
     return (
         jnp.concatenate(dqs, 1)[None],
-        jnp.concatenate(dks, 1)[None],
-        jnp.concatenate(dvs, 1)[None],
+        jnp.concatenate([t[0] for t in totals], 1)[None],
+        jnp.concatenate([t[1] for t in totals], 1)[None],
         weight_grad,
     )
 
@@ -209,7 +255,7 @@
 def solution(mesh):
     rows = P("dp", "seq", None)
     return jax.shard_map(
-        per_device,
+        layer,
         mesh=mesh,
         in_specs=(rows, rows, rows, rows, P("dp", None), P("dp")),
         out_specs=(rows, rows, rows, P("dp", "seq")),

time: 300 us -> 316 us (1.053)
  starting transfers between devices: 26.4 us -> 35.9 us
  waiting for transfers between devices: 158 us -> 151 us
  other arithmetic: 14.5 us -> 20.7 us
  local copies, waits for them, and re-layouts: 11.3 us -> 17 us
  matrix products: 16.4 us -> 20.2 us
    ppermute x0 -> x6, waiting for transfers between devices: none -> 63.2 us  [ring_to(): lax.ppermute(block, axis, [(i, (i + distance) % count) for i in range(cou...]
    reduce_scatter x2 -> x0, waiting for transfers between devices: 43.6 us -> none  [the longest x1 43.6 us: per_device(): column_sums = lax.psum_scatter(term, 'seq', scatter_dimension=1, tiled=True)]
    ppermute x8 -> x6, waiting for transfers between devices: 111 us -> 80.9 us  [shifted(): return lax.ppermute(block, 'seq', route)]
    ppermute x0 -> x6, starting transfers between devices: none -> 11.9 us  [ring_to(): lax.ppermute(block, axis, [(i, (i + distance) % count) for i in range(cou...]
    convert_element_type x10 -> x5, other arithmetic: 5.74 us -> 9.61 us  [the longest x2 6.03 us: layer(): sends.append((t2.astype(f32) + jnp.where(odd, beside, zero)).astype(bf16))]
    dot_general x3 -> x6, matrix products: 16.4 us -> 20.2 us  [dot(): return lax.dot_general(a, b, dims, preferred_element_type=jnp.float32)]
    ppermute x8 -> x6, starting transfers between devices: 23.8 us -> 21.3 us  [shifted(): return lax.ppermute(block, 'seq', route)]
  transfers between devices with their start and end apart: 20 -> 22, of which waited for: 10 -> 14; matrix products, arithmetic and copies ran while one was open for 12% -> 13% of each run, Pallas kernels for 19% -> 7%
where the time goes in v2:
time: 316 us; the launch traced here: 315 us
  waiting for transfers between devices  151 us (48%)
  Pallas kernels  55.2 us (17%)
  starting transfers between devices  35.9 us (11%)
  other arithmetic  20.7 us (7%)
  matrix products  20.2 us (6%)
  local copies, waits for them, and re-layouts  17 us (5%)
  between operations  15 us (5%)
    ppermute x6, waiting for transfers between devices, shifted(): return lax.ppermute(block, 'seq', route)  80.9 us
    ppermute x6, waiting for transfers between devices, ring_to(): lax.ppermute(block, axis, [(i, (i + distance) % count) for i in range(cou...  63.2 us
    pallas_call x2, Pallas kernels, backward(): pl.pallas_call(bwd_kernel, grid_spec=pltpu.PrefetchScalarGridSpec(num_sca...  32.1 us
    pallas_call x2, Pallas kernels, forward(): pl.pallas_call(fwd_kernel, grid_spec=pltpu.PrefetchScalarGridSpec(num_sca...  23 us
    ppermute x6, starting transfers between devices, shifted(): return lax.ppermute(block, 'seq', route)  21.3 us
    dot_general x6, matrix products, dot(): return lax.dot_general(a, b, dims, preferred_element_type=jnp.float32)  20.2 us
    ppermute x6, starting transfers between devices, ring_to(): lax.ppermute(block, axis, [(i, (i + distance) % count) for i in range(cou...  11.9 us
  transfers between devices with their start and end apart: 22, of which 14 were waited for; matrix products, arithmetic and copies ran while one was open for 13% of the time, Pallas kernels for 7%

profile of v2, /device:TPU:0, one launch (start us, length us, event | category | flops | bytes accessed | tf_op | source)
XLA Modules:
  0.0 314.9 jit_solution(2233335979602338250)
XLA Ops:
  7.2 1.5 copy-done
  8.8 1.1 constant_dynamic-slice_fusion
  9.9 1.3 slice.49.k0
  11.2 5.8 %collective-permute-start = (bf16[384,1024]{1,0:T(8,128)(2,1)S(1)}, bf16[384,1024]{1,0:T(8,128)(2,1)}, u32[]{:S(2)}, u32[]{:S(2)}) collective-permute-start(bf16[384,1024]{1,0:T(8,128)(2,1)S(1)} %slice.49.k0), channel_id=1, source_target_pairs={{0,8},{4,12},{8,16},{12,20},{16,24},{20,28},{1,9},{5,13},{9,17},{1... | collective-permute-start | bytes 2359304 | tf_op jit(solution)/shard_map/ppermute | solution.py:141
  17.0 2.1 slice.50.v0
  19.0 3.4 %collective-permute-start.2 = (bf16[384,1024]{1,0:T(8,128)(2,1)}, bf16[384,1024]{1,0:T(8,128)(2,1)}, u32[]{:S(2)}, u32[]{:S(2)}) collective-permute-start(bf16[384,1024]{1,0:T(8,128)(2,1)} %slice.50.v0), channel_id=1, source_target_pairs={{0,8},{4,12},{8,16},{12,20},{16,24},{20,28},{1,9},{5,13},{9,17},{1... | collective-permute-start | bytes 2359304 | tf_op jit(solution)/shard_map/ppermute | solution.py:141
  22.4 11.6 %collective-permute-done.k2 = bf16[384,1024]{1,0:T(8,128)(2,1)} collective-permute-done((bf16[384,1024]{1,0:T(8,128)(2,1)S(1)}, bf16[384,1024]{1,0:T(8,128)(2,1)}, u32[]{:S(2)}, u32[]{:S(2)}) %collective-permute-start) | collective-permute-done | bytes 786464 | tf_op jit(solution)/shard_map/ppermute | solution.py:141
  34.0 1.0 broadcast_select_fusion.3
  35.0 14.8 %collective-permute-done.2.v2 = bf16[384,1024]{1,0:T(8,128)(2,1)} collective-permute-done((bf16[384,1024]{1,0:T(8,128)(2,1)}, bf16[384,1024]{1,0:T(8,128)(2,1)}, u32[]{:S(2)}, u32[]{:S(2)}) %collective-permute-start.2) | collective-permute-done | bytes 786464 | tf_op jit(solution)/shard_map/ppermute | solution.py:141
  49.8 1.1 broadcast_select_fusion.2
  51.0 4.4 %collective-permute-start.4 = (bf16[384,1024]{1,0:T(8,128)(2,1)}, bf16[384,1024]{1,0:T(8,128)(2,1)S(1)}, u32[]{:S(2)}, u32[]{:S(2)}) collective-permute-start(bf16[384,1024]{1,0:T(8,128)(2,1)} %get-tuple-element.56.k0), channel_id=1, source_target_pairs={{0,8},{4,12},{8,16},{12,20},{16,24},{20,28},{1,9},{5,13},{9,17},{1... | collective-permute-start | bytes 2359304 | tf_op jit(solution)/shard_map/ppermute | solution.py:141
  55.5 5.1 %collective-permute-start.5 = (bf16[384,1024]{1,0:T(8,128)(2,1)}, bf16[384,1024]{1,0:T(8,128)(2,1)}, u32[]{:S(2)}, u32[]{:S(2)}) collective-permute-start(bf16[384,1024]{1,0:T(8,128)(2,1)} %get-tuple-element.54.v0), channel_id=1, source_target_pairs={{0,8},{4,12},{8,16},{12,20},{16,24},{20,28},{1,9},{5,13},{9,17},{1... | collective-permute-start | bytes 2359304 | tf_op jit(solution)/shard_map/ppermute | solution.py:141
  60.6 1.3 fusion.31
  61.9 1.0 copy-done.17
  62.8 0.9 copy-done.18
  63.7 11.5 %attn_fwd.2 = (bf16[384,1024]{1,0:T(8,128)(2,1)}, f32[8,1,384]{2,1,0:T(1,128)}) custom-call(s32[1]{0:T(128)} %bitcast.pos, bf16[384,1024]{1,0:T(8,128)(2,1)} %get-tuple-element.57.q_ref, bf16[384,1024]{1,0:T(8,128)(2,1)} %copy-done.11, bf16[384,1024]{1,0:T(8,128)(2,1)} %copy-done.17, bf16[384,1024]{1,0:T(8,128)(2,1)} %collective-permute-done.k2, ...), custom_call_target="tpu_custom_call" | custom-call | flops 5435817984 | bytes 6291456 | tf_op jit(solution)/shard_map/attn_fwd/pallas_call | solution.py:97
  75.3 14.7 %collective-permute-done.5.v2 = bf16[384,1024]{1,0:T(8,128)(2,1)} collective-permute-done((bf16[384,1024]{1,0:T(8,128)(2,1)}, bf16[384,1024]{1,0:T(8,128)(2,1)}, u32[]{:S(2)}, u32[]{:S(2)}) %collective-permute-start.5) | collective-permute-done | bytes 786464 | tf_op jit(solution)/shard_map/ppermute | solution.py:141
  89.9 1.0 broadcast_select_fusion.1
  91.0 1.7 collective-permute-start.7
  92.7 0.9 all-gather.2.cloned.1.call-done
  93.6 0.9 constant_dynamic-update-slice_fusion.1
  94.6 0.2 collective-permute-done.7.v1
  94.8 11.5 %attn_fwd.3 = (bf16[384,1024]{1,0:T(8,128)(2,1)}, f32[8,1,384]{2,1,0:T(1,128)}) custom-call(s32[1]{0:T(128)} %bitcast.pos, bf16[384,1024]{1,0:T(8,128)(2,1)} %get-tuple-element.58.q_ref, bf16[384,1024]{1,0:T(8,128)(2,1)} %get-tuple-element.56.k0, bf16[384,1024]{1,0:T(8,128)(2,1)} %collective-permute-done.6.k1, bf16[384,1024]{1,0:T(8,128)(2,1)} %copy-done.10, ...), custom_call_target="tpu_custom_call" | custom-call | flops 5435817984 | bytes 6291456 | tf_op jit(solution)/shard_map/attn_fwd/pallas_call | solution.py:97
  106.3 2.2 constant_dynamic-update-slice_fusion
  108.5 0.4 collective-permute-start.8
  109.5 1.6 copy.10
  111.1 1.6 broadcast_multiply_fusion
  112.7 1.1 constant_dynamic-slice_fusion.1
  114.1 2.2 collective-permute-done.9
  116.3 3.8 %fusion.12 = f32[2048,256]{1,0:T(8,128)} fusion(s32[]{:T(128)S(6)} %select_n.95, bf16[384,1024]{0,1:T(8,128)(2,1)S(1)} %bitcast.36, bf16[384,1024]{0,1:T(8,128)(2,1)} %collective-permute-done.9, bf16[384,2048]{1,0:T(8,128)(2,1)} %collective-permute-done.8, bf16[384,2048]{1,0:T(8,128)(2,1)S(1)} %copy-done.15), kind=kOutput, calls=%fused_computation.47 | convolution fusion | flops 812384256 | bytes 6815748 | tf_op jit(solution)/shard_map/dot_general | solution.py:22
  120.1 3.5 %convolution_convert_fusion.2 = bf16[2048,256]{1,0:T(8,128)(2,1)} fusion(s32[]{:T(128)S(6)} %select_n.92, bf16[384,1024]{0,1:T(8,128)(2,1)S(1)} %bitcast.37, bf16[384,1024]{0,1:T(8,128)(2,1)} %collective-permute-done.9, bf16[384,2048]{1,0:T(8,128)(2,1)} %collective-permute-done.8, bf16[384,2048]{1,0:T(8,128)(2,1)S(1)} %copy-done.15), kind=kOutput, calls=%fused_computation.18 | convolution fusion | flops 812908544 | bytes 5767172 | tf_op jit(solution)/shard_map/dot_general | solution.py:22
  123.6 3.5 %convolution_convert_fusion.1 = bf16[2048,256]{1,0:T(8,128)(2,1)} fusion(s32[]{:T(128)S(6)} %select_n.93, bf16[384,1024]{0,1:T(8,128)(2,1)S(1)} %bitcast.38, bf16[384,1024]{0,1:T(8,128)(2,1)} %collective-permute-done.9, bf16[384,2048]{1,0:T(8,128)(2,1)} %collective-permute-done.8, bf16[384,2048]{1,0:T(8,128)(2,1)S(1)} %copy-done.15), kind=kOutput, calls=%fused_computation.17 | convolution fusion | flops 812908544 | bytes 5767172 | tf_op jit(solution)/shard_map/dot_general | solution.py:22
  127.0 3.7 %convolution_convert_fusion = bf16[2048,256]{1,0:T(8,128)(2,1)} fusion(s32[]{:T(128)S(6)} %select_n.94, bf16[384,1024]{0,1:T(8,128)(2,1)S(1)} %bitcast.39, bf16[384,1024]{0,1:T(8,128)(2,1)} %collective-permute-done.9, bf16[384,2048]{1,0:T(8,128)(2,1)} %collective-permute-done.8, bf16[384,2048]{1,0:T(8,128)(2,1)S(1)} %copy-done.15), kind=kOutput, calls=%fused_computation.16 | convolution fusion | flops 812908544 | bytes 5767172 | tf_op jit(solution)/shard_map/dot_general | solution.py:22
  130.7 1.8 fusion.32
  132.5 4.1 %add_convert_fusion = bf16[384,2048]{1,0:T(8,128)(2,1)S(1)} fusion(f32[384,2048]{1,0:T(8,128)S(1)} %fusion.32, bf16[2048,1024]{1,0:T(8,128)(2,1)} %collective-permute-done.10, bf16[384,2048]{1,0:T(8,128)(2,1)S(1)} %bitcast_multiply_fusion, s32[]{:T(128)S(6)} %select_n.96), kind=kOutput, calls=%fused_computation.15 | convolution fusion | flops 1612185600 | bytes 9699332 | tf_op jit(solution)/shard_map/dot_general | solution.py:22
  136.6 1.3 fusion.30
  137.9 16.2 %attn_bwd.2 = (bf16[384,1024]{1,0:T(8,128)(2,1)}, bf16[2,384,1024]{2,1,0:T(8,128)(2,1)}, bf16[2,384,1024]{2,1,0:T(8,128)(2,1)}, bf16[2,384,1024]{2,1,0:T(8,128)(2,1)}) custom-call(s32[1]{0:T(128)} %bitcast.pos, bf16[384,1024]{1,0:T(8,128)(2,1)} %get-tuple-element.57.q_ref, bf16[384,1024]{1,0:T(8,128)(2,1)} %copy-done.11, bf16[384,1024]{1,0:T(8,128)(2,1)} %copy-done.17, ...), custom_call_target="tpu_custom_call" | custom-call | flops 10871635968 | bytes 12582912 | tf_op jit(solution)/shard_map/attn_bwd/pallas_call | solution.py:120
  154.1 0.2 collective-permute-start.11
  154.3 3.5 %collective-permute-done.11 = bf16[2,384,1024]{2,1,0:T(8,128)(2,1)S(1)} collective-permute-done((bf16[2,384,1024]{2,1,0:T(8,128)(2,1)}, bf16[2,384,1024]{2,1,0:T(8,128)(2,1)S(1)}, u32[]{:S(2)}, u32[]{:S(2)}) %collective-permute-start.11) | collective-permute-done | bytes 1572896 | tf_op jit(solution)/shard_map/ppermute | solution.py:151
  157.8 3.3 %fusion.1 = bf16[2,384,1024]{2,1,0:T(8,128)(2,1)} fusion(bf16[2,384,1024]{2,1,0:T(8,128)(2,1)S(1)} %collective-permute-done.11, bf16[2,384,1024]{2,1,0:T(8,128)(2,1)} %get-tuple-element.31, pred[]{:T(512)S(6)} %eq.3), kind=kLoop, calls=%fused_computation.5 | loop fusion | flops 3932160 | bytes 4718593 | tf_op jit(solution)/shard_map/convert_element_type | solution.py:227
  161.1 16.0 %attn_bwd.3 = (bf16[384,1024]{1,0:T(8,128)(2,1)}, bf16[2,384,1024]{2,1,0:T(8,128)(2,1)}, bf16[2,384,1024]{2,1,0:T(8,128)(2,1)}, bf16[2,384,1024]{2,1,0:T(8,128)(2,1)}) custom-call(s32[1]{0:T(128)} %bitcast.pos, bf16[384,1024]{1,0:T(8,128)(2,1)} %get-tuple-element.58.q_ref, bf16[384,1024]{1,0:T(8,128)(2,1)} %get-tuple-element.56.k0, ...), custom_call_target="tpu_custom_call" | custom-call | flops 10871635968 | bytes 12582912 | tf_op jit(solution)/shard_map/attn_bwd/pallas_call | solution.py:120
  177.0 0.2 collective-permute-start.13
  177.2 2.5 collective-permute-start.15
  179.7 1.8 collective-permute-start.16
  181.6 2.9 collective-permute-start.17
  184.5 1.3 collective-permute-start.12
  185.8 19.2 %collective-permute-done.15 = bf16[2048,256]{1,0:T(8,128)(2,1)S(1)} collective-permute-done((bf16[2048,256]{1,0:T(8,128)(2,1)}, bf16[2048,256]{1,0:T(8,128)(2,1)S(1)}, u32[]{:S(2)}, u32[]{:S(2)}) %collective-permute-start.15) | collective-permute-done | bytes 1048608 | tf_op jit(solution)/shard_map/ppermute | solution.py:146
  204.9 22.4 %collective-permute-done.16 = bf16[2048,256]{1,0:T(8,128)(2,1)} collective-permute-done((bf16[2048,256]{1,0:T(8,128)(2,1)}, bf16[2048,256]{1,0:T(8,128)(2,1)}, u32[]{:S(2)}, u32[]{:S(2)}) %collective-permute-start.16) | collective-permute-done | bytes 1048608 | tf_op jit(solution)/shard_map/ppermute | solution.py:146
  227.3 2.5 collective-permute-done.17
  229.9 2.8 fusion.9
  232.6 1.3 collective-permute-start.14
  233.9 2.0 convert_add_fusion
  236.1 3.7 %collective-permute-start.20 = (bf16[512,256]{1,0:T(8,128)(2,1)S(1)}, bf16[512,256]{1,0:T(8,128)(2,1)S(1)}, u32[]{:S(2)}, u32[]{:S(2)}) collective-permute-start(bf16[512,256]{1,0:T(8,128)(2,1)S(1)} %get-tuple-element.43), channel_id=1, source_target_pairs={{0,3},{1,0},{2,1},{3,2},{4,7},{5,4},{6,5},{7,6},{8,11},{9,8},{10,9... | collective-permute-start | bytes 786440 | tf_op jit(solution)/shard_map/ppermute | solution.py:146
  239.7 1.0 collective-permute-start.18
  240.8 1.3 maximum_bitcast_fusion
  242.0 4.4 %collective-permute-done.20 = bf16[512,256]{1,0:T(8,128)(2,1)S(1)} collective-permute-done((bf16[512,256]{1,0:T(8,128)(2,1)S(1)}, bf16[512,256]{1,0:T(8,128)(2,1)S(1)}, u32[]{:S(2)}, u32[]{:S(2)}) %collective-permute-start.20) | collective-permute-done | bytes 262176 | tf_op jit(solution)/shard_map/ppermute | solution.py:146
  246.5 14.7 %collective-permute-done.19 = bf16[512,256]{1,0:T(8,128)(2,1)S(1)} collective-permute-done((bf16[512,256]{1,0:T(8,128)(2,1)S(1)}, bf16[512,256]{1,0:T(8,128)(2,1)S(1)}, u32[]{:S(2)}, u32[]{:S(2)}) %collective-permute-start.19) | collective-permute-done | bytes 262176 | tf_op jit(solution)/shard_map/ppermute | solution.py:146
  261.2 0.9 convert_add_fusion.1
  262.1 0.8 collective-permute-done.12
  262.9 1.1 fusion.4
  264.1 39.0 %collective-permute-done.14 = bf16[2,384,1024]{2,1,0:T(8,128)(2,1)S(1)} collective-permute-done((bf16[2,384,1024]{2,1,0:T(8,128)(2,1)S(1)}, bf16[2,384,1024]{2,1,0:T(8,128)(2,1)S(1)}, u32[]{:S(2)}, u32[]{:S(2)}) %collective-permute-start.14) | collective-permute-done | bytes 1572896 | tf_op jit(solution)/shard_map/ppermute | solution.py:141
  303.1 2.5 fusion.7
  305.8 2.0 maximum_bitcast_fusion.1
  307.8 0.3 copy-done.1
  (57 shorter events, 1.1 us)
Async XLA Ops:
  7.2 1.6 copy-start
  7.2 86.4 %all-gather.2.cloned.1.call-start = ((), (), s32[]{:S(2)}) async-start(), calls=%async_computation | async-start | bytes 5242880 | tf_op jit(solution)/shard_map/all_gather | solution.py:179
  9.9 24.1 %copy-start.2 = (bf16[1,384,2048]{2,1,0:T(8,128)(2,1)S(1)}, bf16[1,384,2048]{2,1,0:T(8,128)(2,1)}, u32[]{:S(2)}) copy-start(bf16[1,384,2048]{2,1,0:T(8,128)(2,1)} %param.7) | copy-start | bytes 4718596
  11.2 23.8 %copy-start.11 = (bf16[384,1024]{1,0:T(8,128)(2,1)}, bf16[384,1024]{1,0:T(8,128)(2,1)S(1)}, u32[]{:S(2)}) copy-start(bf16[384,1024]{1,0:T(8,128)(2,1)S(1)} %slice.49.k0) | copy-start | bytes 2359300
  11.2 22.8 %collective-permute-start = (bf16[384,1024]{1,0:T(8,128)(2,1)S(1)}, bf16[384,1024]{1,0:T(8,128)(2,1)}, u32[]{:S(2)}, u32[]{:S(2)}) collective-permute-start(bf16[384,1024]{1,0:T(8,128)(2,1)S(1)} %slice.49.k0), channel_id=1, source_target_pairs={{0,8},{4,12},{8,16},{12,20},{16,24},{20,28},{1,9},{5,13},{9,17},{1... | collective-permute-start | bytes 2359304 | tf_op jit(solution)/shard_map/ppermute | solution.py:141
  19.0 30.8 %collective-permute-start.2 = (bf16[384,1024]{1,0:T(8,128)(2,1)}, bf16[384,1024]{1,0:T(8,128)(2,1)}, u32[]{:S(2)}, u32[]{:S(2)}) collective-permute-start(bf16[384,1024]{1,0:T(8,128)(2,1)} %slice.50.v0), channel_id=1, source_target_pairs={{0,8},{4,12},{8,16},{12,20},{16,24},{20,28},{1,9},{5,13},{9,17},{1... | collective-permute-start | bytes 2359304 | tf_op jit(solution)/shard_map/ppermute | solution.py:141
  22.4 27.4 %copy-start.3 = (bf16[1,384,2048]{2,1,0:T(8,128)(2,1)S(1)}, bf16[1,384,2048]{2,1,0:T(8,128)(2,1)}, u32[]{:S(2)}) copy-start(bf16[1,384,2048]{2,1,0:T(8,128)(2,1)} %param.8) | copy-start | bytes 4718596
  35.0 25.6 %copy-start.7 = (bf16[1,384,2048]{2,1,0:T(8,128)(2,1)S(1)}, bf16[1,384,2048]{2,1,0:T(8,128)(2,1)}, u32[]{:S(2)}) copy-start(bf16[1,384,2048]{2,1,0:T(8,128)(2,1)} %param.6) | copy-start | bytes 4718596
  35.0 26.9 %collective-permute-start.1 = (bf16[384,1024]{1,0:T(8,128)(2,1)S(1)}, bf16[384,1024]{1,0:T(8,128)(2,1)S(1)}, u32[]{:S(2)}, u32[]{:S(2)}) collective-permute-start(bf16[384,1024]{1,0:T(8,128)(2,1)S(1)} %get-tuple-element.55), channel_id=1, source_target_pairs={{0,4},{4,0},{8,12},{12,8},{16,20},{20,16},{24,28},{28,24},{1,5},{5... | collective-permute-start | bytes 2359304 | tf_op jit(solution)/shard_map/ppermute | solution.py:151
  50.9 11.0 %collective-permute-start.3 = (bf16[384,1024]{1,0:T(8,128)(2,1)S(1)}, bf16[384,1024]{1,0:T(8,128)(2,1)S(1)}, u32[]{:S(2)}, u32[]{:S(2)}) collective-permute-start(bf16[384,1024]{1,0:T(8,128)(2,1)S(1)} %get-tuple-element.53), channel_id=1, source_target_pairs={{0,4},{4,0},{8,12},{12,8},{16,20},{20,16},{24,28},{28,24},{1,5},{5... | collective-permute-start | bytes 2359304 | tf_op jit(solution)/shard_map/ppermute | solution.py:151
  51.0 24.2 %collective-permute-start.4 = (bf16[384,1024]{1,0:T(8,128)(2,1)}, bf16[384,1024]{1,0:T(8,128)(2,1)S(1)}, u32[]{:S(2)}, u32[]{:S(2)}) collective-permute-start(bf16[384,1024]{1,0:T(8,128)(2,1)} %get-tuple-element.56.k0), channel_id=1, source_target_pairs={{0,8},{4,12},{8,16},{12,20},{16,24},{20,28},{1,9},{5,13},{9,17},{1... | collective-permute-start | bytes 2359304 | tf_op jit(solution)/shard_map/ppermute | solution.py:141
  55.5 34.5 %collective-permute-start.5 = (bf16[384,1024]{1,0:T(8,128)(2,1)}, bf16[384,1024]{1,0:T(8,128)(2,1)}, u32[]{:S(2)}, u32[]{:S(2)}) collective-permute-start(bf16[384,1024]{1,0:T(8,128)(2,1)} %get-tuple-element.54.v0), channel_id=1, source_target_pairs={{0,8},{4,12},{8,16},{12,20},{16,24},{20,28},{1,9},{5,13},{9,17},{1... | collective-permute-start | bytes 2359304 | tf_op jit(solution)/shard_map/ppermute | solution.py:141
  61.9 1.0 copy-start.17
  62.8 0.9 copy-start.18
  75.2 15.7 %copy-start.4 = (bf16[1,384,2048]{2,1,0:T(8,128)(2,1)S(1)}, bf16[1,384,2048]{2,1,0:T(8,128)(2,1)}, u32[]{:S(2)}) copy-start(bf16[1,384,2048]{2,1,0:T(8,128)(2,1)} %param.8) | copy-start | bytes 4718596
  75.2 15.8 %copy-start.10 = (bf16[384,1024]{1,0:T(8,128)(2,1)}, bf16[384,1024]{1,0:T(8,128)(2,1)S(1)}, u32[]{:S(2)}) copy-start(bf16[384,1024]{1,0:T(8,128)(2,1)S(1)} %collective-permute-done.4.k2) | copy-start | bytes 2359300
  90.9 2.7 copy-start.12
  90.9 3.7 %collective-permute-start.6 = (bf16[384,1024]{1,0:T(8,128)(2,1)}, bf16[384,1024]{1,0:T(8,128)(2,1)}, u32[]{:S(2)}, u32[]{:S(2)}) collective-permute-start(bf16[384,1024]{1,0:T(8,128)(2,1)} %broadcast_select_fusion.1), channel_id=1, source_target_pairs={{0,4},{4,0},{8,12},{12,8},{16,20},{20,16},{24,28},{28,24},{1,5},{5... | collective-permute-start | bytes 2359304 | tf_op jit(solution)/shard_map/ppermute | solution.py:151
  91.0 3.7 %collective-permute-start.7 = (bf16[384,1024]{1,0:T(8,128)(2,1)S(1)}, bf16[384,1024]{1,0:T(8,128)(2,1)}, u32[]{:S(2)}, u32[]{:S(2)}) collective-permute-start(bf16[384,1024]{1,0:T(8,128)(2,1)S(1)} %broadcast_select_fusion), channel_id=1, source_target_pairs={{0,4},{4,0},{8,12},{12,8},{16,20},{20,16},{24,28},{28,24},{1,5},{5... | collective-permute-start | bytes 2359304 | tf_op jit(solution)/shard_map/ppermute | solution.py:151
  93.6 38.9 %collective-permute-start.10 = (bf16[2048,1024]{1,0:T(8,128)(2,1)}, bf16[2048,1024]{1,0:T(8,128)(2,1)}, u32[]{:S(2)}, u32[]{:S(2)}) collective-permute-start(bf16[2048,1024]{1,0:T(8,128)(2,1)} %all-gather.2.cloned.1.call-done), channel_id=1, source_target_pairs={{0,4},{4,0},{8,12},{12,8},{16,20},{20,16},{24,28},{28,24},{1,5},{5... | collective-permute-start | bytes 12582920 | tf_op jit(solution)/shard_map/ppermute | solution.py:151
  106.3 3.2 %copy-start.5 = (bf16[1,384,2048]{2,1,0:T(8,128)(2,1)S(1)}, bf16[1,384,2048]{2,1,0:T(8,128)(2,1)}, u32[]{:S(2)}) copy-start(bf16[1,384,2048]{2,1,0:T(8,128)(2,1)} %param.9) | copy-start | bytes 4718596
  108.5 7.9 %collective-permute-start.8 = (bf16[384,2048]{1,0:T(8,128)(2,1)}, bf16[384,2048]{1,0:T(8,128)(2,1)}, u32[]{:S(2)}, u32[]{:S(2)}) collective-permute-start(bf16[384,2048]{1,0:T(8,128)(2,1)} %constant_dynamic-update-slice_fusion), channel_id=1, source_target_pairs={{0,4},{4,0},{8,12},{12,8},{16,20},{20,16},{24,28},{28,24},{1,5},{5... | collective-permute-start | bytes 4718600 | tf_op jit(solution)/shard_map/ppermute | solution.py:151
  113.7 2.6 collective-permute-start.9
  114.0 2.3 copy-start.15
  127.0 3.7 %copy-start.16 = (bf16[2048,1024]{1,0:T(8,128)(2,1)S(1)}, bf16[2048,1024]{1,0:T(8,128)(2,1)}, u32[]{:S(2)}) copy-start(bf16[2048,1024]{1,0:T(8,128)(2,1)} %all-gather.2.cloned.1.call-done) | copy-start | bytes 12582916
  154.1 3.7 %collective-permute-start.11 = (bf16[2,384,1024]{2,1,0:T(8,128)(2,1)}, bf16[2,384,1024]{2,1,0:T(8,128)(2,1)S(1)}, u32[]{:S(2)}, u32[]{:S(2)}) collective-permute-start(bf16[2,384,1024]{2,1,0:T(8,128)(2,1)} %get-tuple-element.32), channel_id=1, source_target_pairs={{0,4},{4,0},{8,12},{12,8},{16,20},{20,16},{24,28},{28,24},{1,5},{5... | collective-permute-start | bytes 4718600 | tf_op jit(solution)/shard_map/ppermute | solution.py:151
  177.0 52.8 %collective-permute-start.13 = (bf16[2,384,1024]{2,1,0:T(8,128)(2,1)}, bf16[2,384,1024]{2,1,0:T(8,128)(2,1)}, u32[]{:S(2)}, u32[]{:S(2)}) collective-permute-start(bf16[2,384,1024]{2,1,0:T(8,128)(2,1)} %get-tuple-element.37), channel_id=1, source_target_pairs={{0,4},{4,0},{8,12},{12,8},{16,20},{20,16},{24,28},{28,24},{1,5},{5... | collective-permute-start | bytes 4718600 | tf_op jit(solution)/shard_map/ppermute | solution.py:151
  177.2 27.7 %collective-permute-start.15 = (bf16[2048,256]{1,0:T(8,128)(2,1)}, bf16[2048,256]{1,0:T(8,128)(2,1)S(1)}, u32[]{:S(2)}, u32[]{:S(2)}) collective-permute-start(bf16[2048,256]{1,0:T(8,128)(2,1)} %convolution_convert_fusion.2), channel_id=1, source_target_pairs={{0,8},{4,12},{8,16},{12,20},{16,24},{20,28},{24,0},{28,4},{1,9},{5... | collective-permute-start | bytes 3145736 | tf_op jit(solution)/shard_map/ppermute | solution.py:146
  179.7 47.6 %collective-permute-start.16 = (bf16[2048,256]{1,0:T(8,128)(2,1)}, bf16[2048,256]{1,0:T(8,128)(2,1)}, u32[]{:S(2)}, u32[]{:S(2)}) collective-permute-start(bf16[2048,256]{1,0:T(8,128)(2,1)} %convolution_convert_fusion.1), channel_id=1, source_target_pairs={{0,16},{4,20},{8,24},{12,28},{16,0},{20,4},{24,8},{28,12},{1,17},{... | collective-permute-start | bytes 3145736 | tf_op jit(solution)/shard_map/ppermute | solution.py:146
  181.6 48.3 %collective-permute-start.17 = (bf16[2048,256]{1,0:T(8,128)(2,1)}, bf16[2048,256]{1,0:T(8,128)(2,1)}, u32[]{:S(2)}, u32[]{:S(2)}) collective-permute-start(bf16[2048,256]{1,0:T(8,128)(2,1)} %convolution_convert_fusion), channel_id=1, source_target_pairs={{0,24},{4,28},{8,0},{12,4},{16,8},{20,12},{24,16},{28,20},{1,25},{... | collective-permute-start | bytes 3145736 | tf_op jit(solution)/shard_map/ppermute | solution.py:146
  184.5 78.4 %collective-permute-start.12 = (bf16[2,384,1024]{2,1,0:T(8,128)(2,1)}, bf16[2,384,1024]{2,1,0:T(8,128)(2,1)S(1)}, u32[]{:S(2)}, u32[]{:S(2)}) collective-permute-start(bf16[2,384,1024]{2,1,0:T(8,128)(2,1)} %fusion.1), channel_id=1, source_target_pairs={{8,0},{12,4},{16,8},{20,12},{24,16},{28,20},{9,1},{13,5},{17,9},{2... | collective-permute-start | bytes 4718600 | tf_op jit(solution)/shard_map/ppermute | solution.py:141
  229.9 4.1 %copy-start.6 = (f32[2048,256]{1,0:T(8,128)S(1)}, f32[2048,256]{1,0:T(8,128)}, u32[]{:S(2)}) copy-start(f32[2048,256]{1,0:T(8,128)} %fusion.12) | copy-start | bytes 6291460
  232.6 70.5 %collective-permute-start.14 = (bf16[2,384,1024]{2,1,0:T(8,128)(2,1)S(1)}, bf16[2,384,1024]{2,1,0:T(8,128)(2,1)S(1)}, u32[]{:S(2)}, u32[]{:S(2)}) collective-permute-start(bf16[2,384,1024]{2,1,0:T(8,128)(2,1)S(1)} %fusion.9), channel_id=1, source_target_pairs={{8,0},{12,4},{16,8},{20,12},{24,16},{28,20},{9,1},{13,5},{17,9},{2... | collective-permute-start | bytes 4718600 | tf_op jit(solution)/shard_map/ppermute | solution.py:141
  236.0 4.8 %copy-start.13 = (bf16[384,1024]{1,0:T(8,128)(2,1)S(1)}, bf16[384,1024]{1,0:T(8,128)(2,1)}, u32[]{:S(2)}) copy-start(bf16[384,1024]{1,0:T(8,128)(2,1)} %get-tuple-element.29) | copy-start | bytes 2359300
  236.0 4.8 %copy-start.14 = (bf16[384,1024]{1,0:T(8,128)(2,1)S(1)}, bf16[384,1024]{1,0:T(8,128)(2,1)}, u32[]{:S(2)}) copy-start(bf16[384,1024]{1,0:T(8,128)(2,1)} %get-tuple-element.34) | copy-start | bytes 2359300
  236.1 10.4 %collective-permute-start.20 = (bf16[512,256]{1,0:T(8,128)(2,1)S(1)}, bf16[512,256]{1,0:T(8,128)(2,1)S(1)}, u32[]{:S(2)}, u32[]{:S(2)}) collective-permute-start(bf16[512,256]{1,0:T(8,128)(2,1)S(1)} %get-tuple-element.43), channel_id=1, source_target_pairs={{0,3},{1,0},{2,1},{3,2},{4,7},{5,4},{6,5},{7,6},{8,11},{9,8},{10,9... | collective-permute-start | bytes 786440 | tf_op jit(solution)/shard_map/ppermute | solution.py:146
  239.7 21.4 %collective-permute-start.19 = (bf16[512,256]{1,0:T(8,128)(2,1)S(1)}, bf16[512,256]{1,0:T(8,128)(2,1)S(1)}, u32[]{:S(2)}, u32[]{:S(2)}) collective-permute-start(bf16[512,256]{1,0:T(8,128)(2,1)S(1)} %get-tuple-element.44), channel_id=1, source_target_pairs={{0,2},{1,3},{2,0},{3,1},{4,6},{5,7},{6,4},{7,5},{8,10},{9,11},{10,... | collective-permute-start | bytes 786440 | tf_op jit(solution)/shard_map/ppermute | solution.py:146
  239.7 21.4 %collective-permute-start.18 = (bf16[512,256]{1,0:T(8,128)(2,1)S(1)}, bf16[512,256]{1,0:T(8,128)(2,1)S(1)}, u32[]{:S(2)}, u32[]{:S(2)}) collective-permute-start(bf16[512,256]{1,0:T(8,128)(2,1)S(1)} %get-tuple-element.42), channel_id=1, source_target_pairs={{0,1},{1,2},{2,3},{3,0},{4,5},{5,6},{6,7},{7,4},{8,9},{9,10},{10,1... | collective-permute-start | bytes 786440 | tf_op jit(solution)/shard_map/ppermute | solution.py:146
  242.0 20.8 %copy-start.8 = (bf16[2,384,1024]{2,1,0:T(8,128)(2,1)S(1)}, bf16[2,384,1024]{2,1,0:T(8,128)(2,1)}, u32[]{:S(2)}) copy-start(bf16[2,384,1024]{2,1,0:T(8,128)(2,1)} %get-tuple-element.35) | copy-start | bytes 4718596
  264.0 39.2 %copy-start.9 = (bf16[2,384,1024]{2,1,0:T(8,128)(2,1)S(1)}, bf16[2,384,1024]{2,1,0:T(8,128)(2,1)}, u32[]{:S(2)}) copy-start(bf16[2,384,1024]{2,1,0:T(8,128)(2,1)} %get-tuple-element.36) | copy-start | bytes 4718596
  305.8 2.3 copy-start.1
Sparse Core Ops, SparseCore 0:
  10.1 83.4 all-gather.1

commit v3 on v1

v3 whole, which is shorter than its diff:
```python
import functools

import jax
import jax.numpy as jnp
from jax import lax
from jax.experimental import pallas as pl
from jax.experimental.pallas import tpu as pltpu
from jax.sharding import PartitionSpec as P


HEAD_DIM = 128
GROUPS = 2
LOG2E = 1.4426950408889634
NEG = -1e30

NT = (((1,), (1,)), ((), ()))
NN = (((1,), (0,)), ((), ()))
TN = (((0,), (0,)), ((), ()))


def dot(a, b, dims):
    return lax.dot_general(a, b, dims, preferred_element_type=jnp.float32)


def scores_t(k, q, causal):
    s = dot(k, q, NT)
    if causal:
        key_at = lax.broadcasted_iota(jnp.int32, s.shape, 0)
        query_at = lax.broadcasted_iota(jnp.int32, s.shape, 1)
        s = jnp.where(key_at <= query_at, s, NEG)
    return s


def fwd_kernel(pos, q_ref, k0, v0, k1, k2, v1, v2, o_ref, lse_ref):
    c = HEAD_DIM ** (-0.5) * LOG2E
    q = q_ref[...]
    parts = []
    for offset, k in enumerate((k0, k1, k2)):
        parts.append(scores_t(k[...], q, offset == 0))
    tops = [jnp.max(parts[0], axis=0, keepdims=True)]
    for offset in (1, 2):
        off = jnp.where(pos[0] >= offset, 0.0, NEG)
        tops.append(jnp.max(parts[offset], axis=0, keepdims=True) + off)
    top = functools.reduce(jnp.maximum, tops) * c
    total = None
    out = None
    for offset, v in enumerate((v0, v1, v2)):
        off = jnp.where(pos[0] >= offset, 0.0, -NEG)
        e = jnp.exp2(parts[offset] * c - (top + off))
        t = jnp.sum(e, axis=0, keepdims=True)
        o = dot(v[...], e.astype(jnp.bfloat16), TN)
        total = t if total is None else total + t
        out = o if out is None else out + o
    out = out * (1.0 / total)
    o_ref[...] = out.T.astype(jnp.bfloat16)
    lse_ref[0] = top + jnp.log2(total)


def bwd_kernel(pos, q_ref, k0, v0, k1, k2, v1, v2, o_ref, lse_ref, do_ref, *rest):
    dq_ref, t0, t1, t2 = rest[-4:]
    scale = HEAD_DIM ** (-0.5)
    c = scale * LOG2E
    q = q_ref[...]
    do = do_ref[...]
    prod = do.astype(jnp.float32) * o_ref[...].astype(jnp.float32)
    delta = jnp.sum(prod.T, axis=0, keepdims=True)
    lse = lse_ref[0]
    dq = None
    for offset, (k_ref, v_ref, term) in enumerate(((k0, v0, t0), (k1, v1, t1), (k2, v2, t2))):
        k = k_ref[...]
        off = jnp.where(pos[0] >= offset, 0.0, -NEG)
        s = scores_t(k, q, offset == 0)
        p = jnp.exp2(s * c - (lse + off))
        term[1] = dot(p.astype(jnp.bfloat16), do, NN).astype(jnp.bfloat16)
        dp = dot(v_ref[...], do, NT)
        ds = (p * (dp - delta)).astype(jnp.bfloat16)
        term[0] = (dot(ds, q, NN) * scale).astype(jnp.bfloat16)
        part = dot(k, ds, TN)
        dq = part if dq is None else dq + part
    dq_ref[...] = (dq * scale).T.astype(jnp.bfloat16)


def head_specs(tokens, count):
    return [pl.BlockSpec((tokens, HEAD_DIM), lambda h, pos: (0, h))] * count


def spread_specs(tokens, count, group, per):
    def where(h, pos):
        return (0, (h // per) * (per * GROUPS) + group * per + h % per)

    return [pl.BlockSpec((tokens, HEAD_DIM), where)] * count


def lse_spec(tokens):
    return pl.BlockSpec((1, 1, tokens), lambda h, pos: (h, 0, 0))


def forward(pos, group, per, full, k1, k2, v1, v2):
    tokens, width = k1.shape
    heads = width // HEAD_DIM
    pairs = heads * tokens * tokens * 3
    return pl.pallas_call(
        fwd_kernel,
        grid_spec=pltpu.PrefetchScalarGridSpec(
            num_scalar_prefetch=1,
            grid=(heads,),
            in_specs=spread_specs(tokens, 3, group, per) + head_specs(tokens, 4),
            out_specs=head_specs(tokens, 1) + [lse_spec(tokens)],
        ),
        out_shape=[
            jax.ShapeDtypeStruct((tokens, width), jnp.bfloat16),
            jax.ShapeDtypeStruct((heads, 1, tokens), jnp.float32),
        ],
        cost_estimate=pl.CostEstimate(
            flops=pairs * HEAD_DIM * 12, bytes_accessed=tokens * width * 16, transcendentals=pairs
        ),
        name="attn_fwd",
    )(pos, *full, k1, k2, v1, v2)


def backward(pos, group, per, full, k1, k2, v1, v2, o, lse, do, held):
    tokens, width = k1.shape
    heads = width // HEAD_DIM
    pairs = heads * tokens * tokens * 3
    return pl.pallas_call(
        bwd_kernel,
        grid_spec=pltpu.PrefetchScalarGridSpec(
            num_scalar_prefetch=1,
            grid=(heads,),
            in_specs=spread_specs(tokens, 3, group, per)
            + head_specs(tokens, 5)
            + [lse_spec(tokens)]
            + head_specs(tokens, 1)
            + [pl.BlockSpec(memory_space=pl.ANY)] * len(held),
            out_specs=spread_specs(tokens, 1, group, per)
            + [pl.BlockSpec((2, tokens, HEAD_DIM), lambda h, pos: (0, 0, h))] * 3,
        ),
        out_shape=[jax.ShapeDtypeStruct((tokens, width * GROUPS), jnp.bfloat16)]
        + [jax.ShapeDtypeStruct((2, tokens, width), jnp.bfloat16)] * 3,
        cost_estimate=pl.CostEstimate(
            flops=pairs * HEAD_DIM * 24, bytes_accessed=tokens * width * 32, transcendentals=pairs
        ),
        input_output_aliases={11: 0} if held else {},
        name="attn_bwd",
    )(pos, *full, k1, k2, v1, v2, o, lse, do, *held)


def finish_kernel(pos, own_ref, beside_ref, behind_ref, *rest):
    f32 = jnp.float32
    keep = 1 - lax.rem(pos[0], 2)
    for i, out in enumerate(rest[-2:]):
        beside = jnp.where(keep == 1, beside_ref[i].astype(f32), 0.0)
        out[...] = (own_ref[i].astype(f32) + beside + behind_ref[i].astype(f32)).astype(out.dtype)


def finish(pos, group, count, own, beside, behind, held):
    _, tokens, width = own.shape
    sub = width // count
    return pl.pallas_call(
        finish_kernel,
        grid_spec=pltpu.PrefetchScalarGridSpec(
            num_scalar_prefetch=1,
            grid=(count,),
            in_specs=[pl.BlockSpec((2, tokens, sub), lambda c, pos: (0, 0, c))] * 3
            + [pl.BlockSpec(memory_space=pl.ANY)] * len(held),
            out_specs=[pl.BlockSpec((tokens, sub), lambda c, pos: (0, c * GROUPS + group))] * 2,
        ),
        out_shape=[jax.ShapeDtypeStruct((tokens, width * GROUPS), own.dtype)] * 2,
        cost_estimate=pl.CostEstimate(
            flops=6 * tokens * width, bytes_accessed=tokens * width * 16, transcendentals=0
        ),
        input_output_aliases={4: 0, 5: 1} if held else {},
        name="finish",
    )(pos, own, beside, behind, *held)


def shifted(block, distance):
    devices = range(lax.axis_size("seq"))
    route = [(i - distance, i) for i in devices if i - distance in devices]
    return lax.ppermute(block, "seq", route)


def ring_to(block, axis, distance):
    count = lax.axis_size(axis)
    return lax.ppermute(block, axis, [(i, (i + distance) % count) for i in range(count)])


def crossed(block, bit):
    return lax.ppermute(block, "seq", [(i, i ^ bit) for i in range(lax.axis_size("seq"))])


def swapped(block):
    route = [(i, i ^ 1) for i in range(lax.axis_size("seq"))]
    return lax.ppermute(block, "seq", route)


def after(arrays, *earlier):
    return lax.optimization_barrier((*arrays, *earlier))[: len(arrays)]


def layer(queries, keys, values, out_grad, proj_weight, lengths):
    f32, bf16 = jnp.float32, jnp.bfloat16
    tokens, width = queries.shape[1:]
    place = lax.axis_index("seq")
    odd = lax.rem(place, 2) == 1
    pos = place.astype(jnp.int32).reshape(1)
    query_pos = place * tokens + jnp.arange(tokens, dtype=jnp.int32)
    live = (query_pos < lengths[0]).astype(bf16)
    grad_masked = out_grad[0] * live[:, None]

    here, count = lax.axis_index("dp"), lax.axis_size("dp")
    rows = proj_weight.shape[0]
    sub = rows // GROUPS
    per = sub // HEAD_DIM
    full = (queries[0], keys[0], values[0])

    def columns(array, g):
        starts = range(g * sub, width, rows)
        return jnp.concatenate([array[:, at : at + sub] for at in starts], 1)

    near = [(columns(keys[0], g), columns(values[0], g)) for g in range(GROUPS)]
    halo = []
    for k0, v0 in near:
        k2 = shifted(k0, 2)
        halo.append((k2, shifted(v0, 2)))

    half = proj_weight.shape[1] // 2
    parity = lax.rem(place, 2)
    mine = parity * half
    weights = []
    for g in range(GROUPS):
        block = lax.dynamic_slice(proj_weight, (g * sub, mine), (sub, half))
        gathered = lax.all_gather(block, "dp", axis=0, tiled=True)
        weights.append((gathered, swapped(gathered)))
    grad_mine = lax.dynamic_slice_in_dim(grad_masked, mine, half, 1)
    grad_other = lax.dynamic_slice_in_dim(grad_masked, half - mine, half, 1)

    chips = lax.axis_size("seq") // 2
    chip = place // 2
    own = grad_masked.shape[1] // (2 * chips)

    def owned_by(core):
        return jnp.concatenate(
            [
                lax.dynamic_slice_in_dim(grad_masked, (2 * c + core) * own, own, 1)
                for c in range(chips)
            ],
            1,
        )

    grad_pair = jnp.concatenate([owned_by(parity), swapped(owned_by(1 - parity))], 0)

    dqs, terms, returned, grads = [], [], [], []
    sends = []
    for g, ((k0, v0), (k2, v2)) in enumerate(zip(near, halo)):
        if sends:
            k2, v2 = after((k2, v2), sends[-1])
        k1, v1 = jnp.where(odd, k2, k0), jnp.where(odd, v2, v0)
        side = (swapped(k1), k2, swapped(v1), v2)
        o, lse = forward(pos, g, per, full, *side)

        o_pair = jnp.concatenate([o, swapped(o)], 0)
        span = chips // 2 * own
        upper = lax.rem(chip // (chips // 2), 2)

        def product(side_of):
            return dot(o_pair, lax.dynamic_slice_in_dim(grad_pair, side_of * span, span, 1), TN)

        away = product(1 - upper).astype(bf16)
        came = crossed(away, chips)
        (last_grad,) = after((grad_mine,), away)
        kept = product(upper)

        w_mine, w_other = weights[g]
        do = (dot(last_grad, w_mine, NT) + dot(grad_other, w_other, NT)).astype(bf16)
        dq, t0, t1, t2 = backward(pos, g, per, full, *side, o, lse, do, dqs[-1:])
        dqs.append(dq)
        beside = swapped(t1)
        extra = jnp.where(odd, beside.astype(f32), 0.0)
        sends.append((t2.astype(f32) + extra).astype(bf16))
        terms.append((t0, beside))
        returned.append(shifted(sends[-1], -2))

        bit = chips // 2
        (came,) = after((came,), dq)
        kept = kept + came.astype(f32)
        while bit > 1:
            bit //= 2
            span = bit * own
            upper = lax.rem(chip // bit, 2)
            away = lax.dynamic_slice_in_dim(kept, (1 - upper) * span, span, 1).astype(bf16)
            kept = lax.dynamic_slice_in_dim(kept, upper * span, span, 1)
            came = crossed(away, 2 * bit)
            kept = kept + came.astype(f32)
        grads.append(kept)

    shares = []
    for sums in grads:
        share = lax.dynamic_slice_in_dim(sums, here * sub, sub, 0)
        for step in range(1, count):
            at = lax.rem(here + step, count) * sub
            piece = lax.dynamic_slice_in_dim(sums, at, sub, 0).astype(bf16)
            piece = ring_to(piece, "dp", step)
            share = share + piece.astype(f32)
        shares.append(share)

    totals = ()
    for g, (term, behind) in enumerate(zip(terms, returned)):
        totals = finish(pos, g, count, *term, behind, totals)
    key_grad, value_grad = totals
    return (dqs[-1][None], key_grad[None], value_grad[None], jnp.concatenate(shares, 0))


def solution(mesh):
    rows = P("dp", "seq", None)
    return jax.shard_map(
        layer,
        mesh=mesh,
        in_specs=(rows, rows, rows, rows, P("dp", None), P("dp")),
        out_specs=(rows, rows, rows, P("dp", "seq")),
        check_vma=False,
    )
```

time: 300 us -> 338 us (1.13)
  starting transfers between devices: 26.4 us -> 66.9 us
  waiting for transfers between devices: 158 us -> 142 us
  Pallas kernels: 55.4 us -> 64.5 us
    ppermute x0 -> x10, waiting for transfers between devices: none -> 75.4 us  [the longest x4 71.9 us: crossed(): lax.ppermute(block, 'seq', [(i, i ^ bit) for i in range(lax.axis_size('se...]
    ppermute x8 -> x6, waiting for transfers between devices: 111 us -> 56.1 us  [shifted(): return lax.ppermute(block, 'seq', route)]
    ppermute x0 -> x10, starting transfers between devices: none -> 47.5 us  [the longest x4 40.3 us: crossed(): lax.ppermute(block, 'seq', [(i, i ^ bit) for i in range(lax.axis_size('se...]
    reduce_scatter x2 -> x0, waiting for transfers between devices: 43.6 us -> none  [the longest x1 43.6 us: per_device(): column_sums = lax.psum_scatter(term, 'seq', scatter_dimension=1, tiled=True)]
    all_gather x1 -> x2, waiting for transfers between devices: 0.02 us -> 10.1 us  [layer(): gathered = lax.all_gather(block, 'dp', axis=0, tiled=True)]
    pallas_call x0 -> x2, Pallas kernels: none -> 8.56 us  [finish(): pl.pallas_call(finish_kernel, grid_spec=pltpu.PrefetchScalarGridSpec(num_...]
    concatenate x0 -> x7, other arithmetic: none -> 7.89 us  [the longest x4 3.51 us: columns(): return jnp.concatenate([array[:, at:at + sub] for at in starts], 1)]
    ppermute x8 -> x6, starting transfers between devices: 23.8 us -> 17.9 us  [shifted(): return lax.ppermute(block, 'seq', route)]
  transfers between devices with their start and end apart: 20 -> 29, of which waited for: 10 -> 11; matrix products, arithmetic and copies ran while one was open for 12% -> 11% of each run, Pallas kernels for 19% -> 8%
where the time goes in v3:
time: 338 us; the launch traced here: 337 us
  waiting for transfers between devices  142 us (42%)
  starting transfers between devices  66.9 us (20%)
  Pallas kernels  64.5 us (19%)
  matrix products  18.6 us (6%)
  other arithmetic  16.1 us (5%)
  between operations  15.4 us (5%)
  local copies, waits for them, and re-layouts  14.1 us (4%)
    ppermute x4, waiting for transfers between devices, crossed(): lax.ppermute(block, 'seq', [(i, i ^ bit) for i in range(lax.axis_size('se...  71.9 us
    ppermute x6, waiting for transfers between devices, shifted(): return lax.ppermute(block, 'seq', route)  56.1 us
    ppermute x4, starting transfers between devices, crossed(): lax.ppermute(block, 'seq', [(i, i ^ bit) for i in range(lax.axis_size('se...  40.3 us
    pallas_call x2, Pallas kernels, backward(): pl.pallas_call(bwd_kernel, grid_spec=pltpu.PrefetchScalarGridSpec(num_sca...  32.4 us
    pallas_call x2, Pallas kernels, forward(): pl.pallas_call(fwd_kernel, grid_spec=pltpu.PrefetchScalarGridSpec(num_sca...  23.5 us
    dot_general x8, matrix products, dot(): return lax.dot_general(a, b, dims, preferred_element_type=jnp.float32)  18.6 us
    ppermute x6, starting transfers between devices, shifted(): return lax.ppermute(block, 'seq', route)  17.9 us
    all_gather x2, waiting for transfers between devices, layer(): gathered = lax.all_gather(block, 'dp', axis=0, tiled=True)  10.1 us
  transfers between devices with their start and end apart: 29, of which 11 were waited for; matrix products, arithmetic and copies ran while one was open for 11% of the time, Pallas kernels for 8%

profile of v3, /device:TPU:0, one launch (start us, length us, event | category | flops | bytes accessed | tf_op | source)
XLA Modules:
  0.0 337.1 jit_solution(12322966518993505990)
XLA Ops:
  7.2 2.3 constant_dynamic-slice_fusion.10
  9.7 0.9 fusion.13
  10.5 1.0 pad_maximum_fusion.4
  11.5 5.8 %collective-permute-start.4 = (bf16[384,1024]{1,0:T(8,128)(2,1)}, bf16[384,1024]{1,0:T(8,128)(2,1)}, u32[]{:S(2)}, u32[]{:S(2)}) collective-permute-start(bf16[384,1024]{1,0:T(8,128)(2,1)} %pad_maximum_fusion.4), channel_id=1, source_target_pairs={{0,8},{4,12},{8,16},{12,20},{16,24},{20,28},{1,9},{5,13},{9,17},{1... | collective-permute-start | bytes 2359304 | tf_op jit(solution)/shard_map/ppermute | solution.py:180
  17.3 1.0 fusion.14
  18.2 1.0 pad_maximum_fusion.3
  19.2 2.6 collective-permute-start.2
  22.5 12.2 %collective-permute-done.4.v2 = bf16[384,1024]{1,0:T(8,128)(2,1)} collective-permute-done((bf16[384,1024]{1,0:T(8,128)(2,1)}, bf16[384,1024]{1,0:T(8,128)(2,1)}, u32[]{:S(2)}, u32[]{:S(2)}) %collective-permute-start.4) | collective-permute-done | bytes 786464 | tf_op jit(solution)/shard_map/ppermute | solution.py:180
  34.9 15.4 %collective-permute-done.2.k2 = bf16[384,1024]{1,0:T(8,128)(2,1)S(1)} collective-permute-done((bf16[384,1024]{1,0:T(8,128)(2,1)}, bf16[384,1024]{1,0:T(8,128)(2,1)S(1)}, u32[]{:S(2)}, u32[]{:S(2)}) %collective-permute-start.2) | collective-permute-done | bytes 786464 | tf_op jit(solution)/shard_map/ppermute | solution.py:180
  50.3 1.1 broadcast_select_fusion.3
  51.7 1.2 constant_dynamic-slice_fusion.8
  52.9 5.6 %all-gather.3.cloned.1.call-done = bf16[1024,1024]{1,0:T(8,128)(2,1)} async-done(((bf16[256,1024]{1,0:T(8,128)(2,1)}), bf16[1024,1024]{1,0:T(8,128)(2,1)}) %all-gather.3.cloned.1.call-update) | async-done | bytes 2097168 | tf_op jit(solution)/shard_map/all_gather | solution.py:233
  58.5 2.2 pad_maximum_fusion.5
  60.7 0.5 collective-permute-start.7
  61.3 11.7 %attn_fwd.2 = (bf16[384,1024]{1,0:T(8,128)(2,1)}, f32[8,1,384]{2,1,0:T(1,128)}) custom-call(s32[1]{0:T(128)} %bitcast.pos, bf16[384,2048]{1,0:T(8,128)(2,1)} %bitcast.33, bf16[384,2048]{1,0:T(8,128)(2,1)} %bitcast.21, bf16[384,2048]{1,0:T(8,128)(2,1)} %bitcast.26, bf16[384,1024]{1,0:T(8,128)(2,1)} %collective-permute-done.3.k1, ...), custom_call_target="tpu_custom_call" | custom-call | flops 5435817984 | bytes 6291456 | tf_op jit(solution)/shard_map/attn_fwd/pallas_call | solution.py:102
  73.2 0.7 copy-done.23
  74.1 0.3 copy-done.26
  74.4 1.4 pad_maximum_fusion
  75.9 1.7 constant_dynamic-update-slice_fusion
  77.6 1.1 copy-done.30
  78.7 2.0 convolution_convert_fusion.1
  80.7 1.0 fusion.15
  81.7 3.6 %add_convert_fusion.3.do_ref = bf16[384,1024]{1,0:T(8,128)(2,1)} fusion(f32[384,1024]{1,0:T(8,128)S(1)} %fusion.15, bf16[1024,1024]{1,0:T(8,128)(2,1)} %collective-permute-done.8, bf16[384,2048]{1,0:T(8,128)(2,1)S(1)} %bitcast_multiply_fusion, s32[]{:T(128)S(6)} %select_n.122), kind=kOutput, calls=%fused_computation.7 | convolution fusion | flops 806092800 | bytes 5242884 | tf_op jit(solution)/shard_map/dot_general | solution.py:22
  85.3 16.2 %attn_bwd.2 = (bf16[384,2048]{1,0:T(8,128)(2,1)}, bf16[2,384,1024]{2,1,0:T(8,128)(2,1)}, bf16[2,384,1024]{2,1,0:T(8,128)(2,1)}, bf16[2,384,1024]{2,1,0:T(8,128)(2,1)}) custom-call(s32[1]{0:T(128)} %bitcast.pos, bf16[384,2048]{1,0:T(8,128)(2,1)} %bitcast.34, bf16[384,2048]{1,0:T(8,128)(2,1)} %bitcast.22, bf16[384,2048]{1,0:T(8,128)(2,1)} %bitcast.27, ...), custom_call_target="tpu_custom_call" | custom-call | flops 10871635968 | bytes 12582912 | tf_op jit(solution)/shard_map/attn_bwd/pallas_call | solution.py:125
  101.7 1.5 pad_maximum_fusion.1
  103.1 3.4 %collective-permute-start = (bf16[384,1024]{1,0:T(8,128)(2,1)S(1)}, bf16[384,1024]{1,0:T(8,128)(2,1)S(1)}, u32[]{:S(2)}, u32[]{:S(2)}) collective-permute-start(bf16[384,1024]{1,0:T(8,128)(2,1)S(1)} %pad_maximum_fusion.1), channel_id=1, source_target_pairs={{0,8},{4,12},{8,16},{12,20},{16,24},{20,28},{1,9},{5,13},{9,17},{1... | collective-permute-start | bytes 2359304 | tf_op jit(solution)/shard_map/ppermute | solution.py:180
  106.7 3.6 %collective-permute-start.1 = (bf16[384,1024]{1,0:T(8,128)(2,1)S(1)}, bf16[384,1024]{1,0:T(8,128)(2,1)S(1)}, u32[]{:S(2)}, u32[]{:S(2)}) collective-permute-start(bf16[384,1024]{1,0:T(8,128)(2,1)S(1)} %pad_maximum_fusion.2), channel_id=1, source_target_pairs={{0,8},{4,12},{8,16},{12,20},{16,24},{20,28},{1,9},{5,13},{9,17},{1... | collective-permute-start | bytes 2359304 | tf_op jit(solution)/shard_map/ppermute | solution.py:180
  110.3 1.9 add_convert_fusion.1
  112.2 12.2 %collective-permute-done.k2 = bf16[384,1024]{1,0:T(8,128)(2,1)S(1)} collective-permute-done((bf16[384,1024]{1,0:T(8,128)(2,1)S(1)}, bf16[384,1024]{1,0:T(8,128)(2,1)S(1)}, u32[]{:S(2)}, u32[]{:S(2)}) %collective-permute-start) | collective-permute-done | bytes 786464 | tf_op jit(solution)/shard_map/ppermute | solution.py:180
  124.4 16.4 %collective-permute-done.1.v2 = bf16[384,1024]{1,0:T(8,128)(2,1)S(1)} collective-permute-done((bf16[384,1024]{1,0:T(8,128)(2,1)S(1)}, bf16[384,1024]{1,0:T(8,128)(2,1)S(1)}, u32[]{:S(2)}, u32[]{:S(2)}) %collective-permute-start.1) | collective-permute-done | bytes 786464 | tf_op jit(solution)/shard_map/ppermute | solution.py:180
  141.7 0.3 collective-permute-start.10
  142.0 4.4 %all-gather.5.cloned.1.call-done = bf16[1024,1024]{1,0:T(8,128)(2,1)} async-done(((bf16[256,1024]{1,0:T(8,128)(2,1)}), bf16[1024,1024]{1,0:T(8,128)(2,1)}) %all-gather.5.cloned.1.call-update) | async-done | bytes 2097168 | tf_op jit(solution)/shard_map/all_gather | solution.py:233
  146.4 1.5 collective-permute-start.17
  147.9 11.7 %attn_fwd.3 = (bf16[384,1024]{1,0:T(8,128)(2,1)}, f32[8,1,384]{2,1,0:T(1,128)}) custom-call(s32[1]{0:T(128)} %bitcast.pos, bf16[384,2048]{1,0:T(8,128)(2,1)} %bitcast.35, bf16[384,2048]{1,0:T(8,128)(2,1)} %bitcast.23, bf16[384,2048]{1,0:T(8,128)(2,1)} %bitcast.28, bf16[384,1024]{1,0:T(8,128)(2,1)} %collective-permute-done.10.k1, ...), custom_call_target="tpu_custom_call" | custom-call | flops 5435817984 | bytes 6291456 | tf_op jit(solution)/shard_map/attn_fwd/pallas_call | solution.py:102
  159.8 12.4 %collective-permute-done.17 = bf16[1024,512]{1,0:T(8,128)(2,1)} collective-permute-done((bf16[1024,512]{1,0:T(8,128)(2,1)}, bf16[1024,512]{1,0:T(8,128)(2,1)}, u32[]{:S(2)}, u32[]{:S(2)}) %collective-permute-start.17) | collective-permute-done | bytes 1048608 | tf_op jit(solution)/shard_map/ppermute | solution.py:189
  172.3 1.3 constant_dynamic-update-slice_fusion.3
  173.9 2.0 convolution_convert_fusion
  176.0 0.7 copy-done.34
  176.7 1.0 fusion.16
  177.7 3.5 %add_convert_fusion.2.do_ref = bf16[384,1024]{1,0:T(8,128)(2,1)} fusion(f32[384,1024]{1,0:T(8,128)S(1)} %fusion.16, bf16[1024,1024]{1,0:T(8,128)(2,1)} %collective-permute-done.13, bf16[384,2048]{1,0:T(8,128)(2,1)S(1)} %bitcast_multiply_fusion, s32[]{:T(128)S(6)} %select_n.122), kind=kOutput, calls=%fused_computation.6 | convolution fusion | flops 806092800 | bytes 5242884 | tf_op jit(solution)/shard_map/dot_general | solution.py:22
  181.3 16.2 %attn_bwd.3 = (bf16[384,2048]{1,0:T(8,128)(2,1)}, bf16[2,384,1024]{2,1,0:T(8,128)(2,1)}, bf16[2,384,1024]{2,1,0:T(8,128)(2,1)}, bf16[2,384,1024]{2,1,0:T(8,128)(2,1)}) custom-call(s32[1]{0:T(128)} %bitcast.pos, bf16[384,2048]{1,0:T(8,128)(2,1)} %bitcast.36, bf16[384,2048]{1,0:T(8,128)(2,1)} %bitcast.24, ...), custom_call_target="tpu_custom_call", output_to_operand_aliasing={{0}: (11, {})} | custom-call | flops 10871635968 | bytes 12582912 | tf_op jit(solution)/shard_map/attn_bwd/pallas_call | solution.py:125
  197.6 1.5 collective-permute-start.22
  199.1 3.1 convert_add_fusion.1
  202.2 1.0 dynamic-slice_convert_fusion.1
  203.2 1.5 collective-permute-start.18
  204.6 1.3 collective-permute-start.16
  205.9 17.5 %collective-permute-done.22 = bf16[1024,512]{1,0:T(8,128)(2,1)} collective-permute-done((bf16[1024,512]{1,0:T(8,128)(2,1)}, bf16[1024,512]{1,0:T(8,128)(2,1)}, u32[]{:S(2)}, u32[]{:S(2)}) %collective-permute-start.22) | collective-permute-done | bytes 1048608 | tf_op jit(solution)/shard_map/ppermute | solution.py:189
  223.4 2.4 convert_add_fusion
  225.9 2.4 add_convert_fusion
  228.2 1.3 collective-permute-start.15
  229.6 35.9 %collective-permute-start.23 = (bf16[1024,256]{1,0:T(8,128)(2,1)S(1)}, bf16[1024,256]{1,0:T(8,128)(2,1)S(1)}, u32[]{:S(2)}, u32[]{:S(2)}) collective-permute-start(bf16[1024,256]{1,0:T(8,128)(2,1)S(1)} %dynamic-slice_convert_fusion), channel_id=1, source_target_pairs={{0,8},{4,12},{8,0},{12,4},{16,24},{20,28},{24,16},{28,20},{1,9},{5... | collective-permute-start | bytes 1572872 | tf_op jit(solution)/shard_map/ppermute | solution.py:189
  265.5 1.6 convert_add_fusion.3
  267.4 1.6 collective-permute-start.20
  269.0 41.9 %collective-permute-done.23 = bf16[1024,256]{1,0:T(8,128)(2,1)S(1)} collective-permute-done((bf16[1024,256]{1,0:T(8,128)(2,1)S(1)}, bf16[1024,256]{1,0:T(8,128)(2,1)S(1)}, u32[]{:S(2)}, u32[]{:S(2)}) %collective-permute-start.23) | collective-permute-done | bytes 524320 | tf_op jit(solution)/shard_map/ppermute | solution.py:189
  310.9 1.2 collective-permute-start.21
  312.2 0.7 dynamic-slice_convert_fusion.4
  312.9 0.9 collective-permute-start.24
  313.8 1.2 collective-permute-start.25
  315.0 3.1 collective-permute-done.21
  318.1 2.2 collective-permute-start.26
  320.4 4.3 %finish.2 = (bf16[384,2048]{1,0:T(8,128)(2,1)}, bf16[384,2048]{1,0:T(8,128)(2,1)}) custom-call(s32[1]{0:T(128)} %bitcast.pos, bf16[2,384,1024]{2,1,0:T(8,128)(2,1)} %get-tuple-element.41.own_ref, bf16[2,384,1024]{2,1,0:T(8,128)(2,1)} %copy-done, bf16[2,384,1024]{2,1,0:T(8,128)(2,1)} %collective-permute-done.16.behind_ref), custom_call_target="tpu_custom_call" | custom-call | flops 2359296 | bytes 6291456 | tf_op jit(solution)/shard_map/finish/pallas_call | solution.py:159
  324.7 0.4 collective-permute-done.25
  325.1 0.8 pad_maximum_fusion.6
  325.9 4.3 %finish.3 = (bf16[384,2048]{1,0:T(8,128)(2,1)}, bf16[384,2048]{1,0:T(8,128)(2,1)}) custom-call(s32[1]{0:T(128)} %bitcast.pos, bf16[2,384,1024]{2,1,0:T(8,128)(2,1)} %get-tuple-element.38.own_ref, bf16[2,384,1024]{2,1,0:T(8,128)(2,1)} %copy-done.1, ...), custom_call_target="tpu_custom_call", output_to_operand_aliasing={{0}: (4, {}), {1}: (5, {})} | custom-call | flops 2359296 | bytes 6291456 | tf_op jit(solution)/shard_map/finish/pallas_call | solution.py:159
  (112 shorter events, 3.4 us)
Async XLA Ops:
  7.2 2.5 copy-start.13
  7.2 51.4 %all-gather.3.cloned.1.call-start = ((), (), s32[]{:S(2)}) async-start(), calls=%async_computation | async-start | bytes 2621440 | tf_op jit(solution)/shard_map/all_gather | solution.py:233
  9.6 136.8 %all-gather.5.cloned.1.call-start = ((), (), s32[]{:S(2)}) async-start(), calls=%async_computation.1 | async-start | bytes 2621440 | tf_op jit(solution)/shard_map/all_gather | solution.py:233
  10.5 6.7 %copy-start.12 = (bf16[1,384,2048]{2,1,0:T(8,128)(2,1)S(1)}, bf16[1,384,2048]{2,1,0:T(8,128)(2,1)}, u32[]{:S(2)}) copy-start(bf16[1,384,2048]{2,1,0:T(8,128)(2,1)} %param.7) | copy-start | bytes 4718596
  11.5 23.1 %collective-permute-start.4 = (bf16[384,1024]{1,0:T(8,128)(2,1)}, bf16[384,1024]{1,0:T(8,128)(2,1)}, u32[]{:S(2)}, u32[]{:S(2)}) collective-permute-start(bf16[384,1024]{1,0:T(8,128)(2,1)} %pad_maximum_fusion.4), channel_id=1, source_target_pairs={{0,8},{4,12},{8,16},{12,20},{16,24},{20,28},{1,9},{5,13},{9,17},{1... | collective-permute-start | bytes 2359304 | tf_op jit(solution)/shard_map/ppermute | solution.py:180
  19.2 31.1 %collective-permute-start.2 = (bf16[384,1024]{1,0:T(8,128)(2,1)}, bf16[384,1024]{1,0:T(8,128)(2,1)S(1)}, u32[]{:S(2)}, u32[]{:S(2)}) collective-permute-start(bf16[384,1024]{1,0:T(8,128)(2,1)} %pad_maximum_fusion.3), channel_id=1, source_target_pairs={{0,8},{4,12},{8,16},{12,20},{16,24},{20,28},{1,9},{5,13},{9,17},{1... | collective-permute-start | bytes 2359304 | tf_op jit(solution)/shard_map/ppermute | solution.py:180
  34.8 16.6 %copy-start.11 = (bf16[1,384,2048]{2,1,0:T(8,128)(2,1)S(1)}, bf16[1,384,2048]{2,1,0:T(8,128)(2,1)}, u32[]{:S(2)}) copy-start(bf16[1,384,2048]{2,1,0:T(8,128)(2,1)} %param.9) | copy-start | bytes 4718596
  34.9 26.4 %collective-permute-start.5 = (bf16[384,1024]{1,0:T(8,128)(2,1)S(1)}, bf16[384,1024]{1,0:T(8,128)(2,1)}, u32[]{:S(2)}, u32[]{:S(2)}) collective-permute-start(bf16[384,1024]{1,0:T(8,128)(2,1)S(1)} %broadcast_select_fusion.2), channel_id=1, source_target_pairs={{0,4},{4,0},{8,12},{12,8},{16,20},{20,16},{24,28},{28,24},{1,5},{5... | collective-permute-start | bytes 2359304 | tf_op jit(solution)/shard_map/ppermute | solution.py:194
  50.3 1.3 copy-start.20
  51.5 9.8 %collective-permute-start.3 = (bf16[384,1024]{1,0:T(8,128)(2,1)}, bf16[384,1024]{1,0:T(8,128)(2,1)}, u32[]{:S(2)}, u32[]{:S(2)}) collective-permute-start(bf16[384,1024]{1,0:T(8,128)(2,1)} %broadcast_select_fusion.3), channel_id=1, source_target_pairs={{0,4},{4,0},{8,12},{12,8},{16,20},{20,16},{24,28},{28,24},{1,5},{5... | collective-permute-start | bytes 2359304 | tf_op jit(solution)/shard_map/ppermute | solution.py:194
  58.5 23.2 %collective-permute-start.8 = (bf16[1024,1024]{1,0:T(8,128)(2,1)}, bf16[1024,1024]{1,0:T(8,128)(2,1)}, u32[]{:S(2)}, u32[]{:S(2)}) collective-permute-start(bf16[1024,1024]{1,0:T(8,128)(2,1)} %all-gather.3.cloned.1.call-done), channel_id=1, source_target_pairs={{0,4},{4,0},{8,12},{12,8},{16,20},{20,16},{24,28},{28,24},{1,5},{5... | collective-permute-start | bytes 6291464 | tf_op jit(solution)/shard_map/ppermute | solution.py:194
  60.7 12.5 %collective-permute-start.7 = (bf16[384,1024]{1,0:T(8,128)(2,1)}, bf16[384,1024]{1,0:T(8,128)(2,1)}, u32[]{:S(2)}, u32[]{:S(2)}) collective-permute-start(bf16[384,1024]{1,0:T(8,128)(2,1)} %pad_maximum_fusion.5), channel_id=1, source_target_pairs={{0,4},{4,0},{8,12},{12,8},{16,20},{20,16},{24,28},{28,24},{1,5},{5... | collective-permute-start | bytes 2359304 | tf_op jit(solution)/shard_map/ppermute | solution.py:194
  73.0 0.9 copy-start.23
  73.0 1.0 copy-start.24
  73.0 1.2 copy-start.25
  73.0 1.4 copy-start.26
  73.0 2.9 collective-permute-start.6
  73.2 7.5 %copy-start.27 = (bf16[384,1024]{1,0:T(8,128)(2,1)}, bf16[384,1024]{1,0:T(8,128)(2,1)S(1)}, u32[]{:S(2)}) copy-start(bf16[384,1024]{1,0:T(8,128)(2,1)S(1)} %constant_dynamic-slice_fusion.9) | copy-start | bytes 2359300
  74.4 1.4 copy-start.29
  75.8 1.8 copy-start.14
  77.6 1.1 copy-start.30
  78.7 2.0 copy-start.33
  101.5 8.7 %collective-permute-start.9 = (bf16[2,384,1024]{2,1,0:T(8,128)(2,1)}, bf16[2,384,1024]{2,1,0:T(8,128)(2,1)S(1)}, u32[]{:S(2)}, u32[]{:S(2)}) collective-permute-start(bf16[2,384,1024]{2,1,0:T(8,128)(2,1)} %get-tuple-element.30), channel_id=1, source_target_pairs={{0,4},{4,0},{8,12},{12,8},{16,20},{20,16},{24,28},{28,24},{1,5},{5... | collective-permute-start | bytes 4718600 | tf_op jit(solution)/shard_map/ppermute | solution.py:194
  101.6 4.9 %copy-start.2 = (bf16[384,256]{1,0:T(8,128)(2,1)S(1)}, bf16[384,256]{1,0:T(8,128)(2,1)}, u32[]{:S(2)}) copy-start(bf16[384,256]{1,0:T(8,128)(2,1)} %get-tuple-element.64) | copy-start | bytes 589828
  101.6 4.9 %copy-start.3 = (bf16[384,256]{1,0:T(8,128)(2,1)S(1)}, bf16[384,256]{1,0:T(8,128)(2,1)}, u32[]{:S(2)}) copy-start(bf16[384,256]{1,0:T(8,128)(2,1)} %get-tuple-element.65) | copy-start | bytes 589828
  101.6 8.6 %copy-start.10 = (bf16[2,384,1024]{2,1,0:T(8,128)(2,1)S(1)}, bf16[2,384,1024]{2,1,0:T(8,128)(2,1)}, u32[]{:S(2)}) copy-start(bf16[2,384,1024]{2,1,0:T(8,128)(2,1)} %get-tuple-element.29) | copy-start | bytes 4718596
  103.1 21.3 %collective-permute-start = (bf16[384,1024]{1,0:T(8,128)(2,1)S(1)}, bf16[384,1024]{1,0:T(8,128)(2,1)S(1)}, u32[]{:S(2)}, u32[]{:S(2)}) collective-permute-start(bf16[384,1024]{1,0:T(8,128)(2,1)S(1)} %pad_maximum_fusion.1), channel_id=1, source_target_pairs={{0,8},{4,12},{8,16},{12,20},{16,24},{20,28},{1,9},{5,13},{9,17},{1... | collective-permute-start | bytes 2359304 | tf_op jit(solution)/shard_map/ppermute | solution.py:180
  106.7 34.1 %collective-permute-start.1 = (bf16[384,1024]{1,0:T(8,128)(2,1)S(1)}, bf16[384,1024]{1,0:T(8,128)(2,1)S(1)}, u32[]{:S(2)}, u32[]{:S(2)}) collective-permute-start(bf16[384,1024]{1,0:T(8,128)(2,1)S(1)} %pad_maximum_fusion.2), channel_id=1, source_target_pairs={{0,8},{4,12},{8,16},{12,20},{16,24},{20,28},{1,9},{5,13},{9,17},{1... | collective-permute-start | bytes 2359304 | tf_op jit(solution)/shard_map/ppermute | solution.py:180
  110.3 2.0 copy-start
  112.2 28.9 %copy-start.4 = (bf16[384,256]{1,0:T(8,128)(2,1)S(1)}, bf16[384,256]{1,0:T(8,128)(2,1)}, u32[]{:S(2)}) copy-start(bf16[384,256]{1,0:T(8,128)(2,1)} %get-tuple-element.70) | copy-start | bytes 589828
  112.2 28.9 %copy-start.5 = (bf16[384,256]{1,0:T(8,128)(2,1)S(1)}, bf16[384,256]{1,0:T(8,128)(2,1)}, u32[]{:S(2)}) copy-start(bf16[384,256]{1,0:T(8,128)(2,1)} %get-tuple-element.71) | copy-start | bytes 589828
  112.2 28.9 %copy-start.6 = (bf16[384,256]{1,0:T(8,128)(2,1)S(1)}, bf16[384,256]{1,0:T(8,128)(2,1)}, u32[]{:S(2)}) copy-start(bf16[384,256]{1,0:T(8,128)(2,1)} %get-tuple-element.72) | copy-start | bytes 589828
  112.2 28.9 %copy-start.7 = (bf16[384,256]{1,0:T(8,128)(2,1)S(1)}, bf16[384,256]{1,0:T(8,128)(2,1)}, u32[]{:S(2)}) copy-start(bf16[384,256]{1,0:T(8,128)(2,1)} %get-tuple-element.73) | copy-start | bytes 589828
  124.4 17.0 %copy-start.21 = (bf16[384,1024]{1,0:T(8,128)(2,1)}, bf16[384,1024]{1,0:T(8,128)(2,1)S(1)}, u32[]{:S(2)}) copy-start(bf16[384,1024]{1,0:T(8,128)(2,1)S(1)} %collective-permute-done.k2) | copy-start | bytes 2359300
  140.8 0.9 copy-start.22
  141.0 6.8 %collective-permute-start.11 = (bf16[384,1024]{1,0:T(8,128)(2,1)S(1)}, bf16[384,1024]{1,0:T(8,128)(2,1)}, u32[]{:S(2)}, u32[]{:S(2)}) collective-permute-start(bf16[384,1024]{1,0:T(8,128)(2,1)S(1)} %broadcast_select_fusion), channel_id=1, source_target_pairs={{0,4},{4,0},{8,12},{12,8},{16,20},{20,16},{24,28},{28,24},{1,5},{5... | collective-permute-start | bytes 2359304 | tf_op jit(solution)/shard_map/ppermute | solution.py:194
  141.7 6.2 %collective-permute-start.10 = (bf16[384,1024]{1,0:T(8,128)(2,1)S(1)}, bf16[384,1024]{1,0:T(8,128)(2,1)}, u32[]{:S(2)}, u32[]{:S(2)}) collective-permute-start(bf16[384,1024]{1,0:T(8,128)(2,1)S(1)} %broadcast_select_fusion.1), channel_id=1, source_target_pairs={{0,4},{4,0},{8,12},{12,8},{16,20},{20,16},{24,28},{28,24},{1,5},{5... | collective-permute-start | bytes 2359304 | tf_op jit(solution)/shard_map/ppermute | solution.py:194
  146.4 31.3 %collective-permute-start.13 = (bf16[1024,1024]{1,0:T(8,128)(2,1)}, bf16[1024,1024]{1,0:T(8,128)(2,1)}, u32[]{:S(2)}, u32[]{:S(2)}) collective-permute-start(bf16[1024,1024]{1,0:T(8,128)(2,1)} %all-gather.5.cloned.1.call-done), channel_id=1, source_target_pairs={{0,4},{4,0},{8,12},{12,8},{16,20},{20,16},{24,28},{28,24},{1,5},{5... | collective-permute-start | bytes 6291464 | tf_op jit(solution)/shard_map/ppermute | solution.py:194
  146.4 25.9 %collective-permute-start.17 = (bf16[1024,512]{1,0:T(8,128)(2,1)}, bf16[1024,512]{1,0:T(8,128)(2,1)}, u32[]{:S(2)}, u32[]{:S(2)}) collective-permute-start(bf16[1024,512]{1,0:T(8,128)(2,1)} %convolution_convert_fusion.1), channel_id=1, source_target_pairs={{0,16},{4,20},{8,24},{12,28},{16,0},{20,4},{24,8},{28,12},{1,17},{... | collective-permute-start | bytes 3145736 | tf_op jit(solution)/shard_map/ppermute | solution.py:189
  159.6 14.0 %collective-permute-start.12 = (bf16[384,1024]{1,0:T(8,128)(2,1)}, bf16[384,1024]{1,0:T(8,128)(2,1)S(1)}, u32[]{:S(2)}, u32[]{:S(2)}) collective-permute-start(bf16[384,1024]{1,0:T(8,128)(2,1)} %get-tuple-element.33.o_ref), channel_id=1, source_target_pairs={{0,4},{4,0},{8,12},{12,8},{16,20},{20,16},{24,28},{28,24},{1,5},{5... | collective-permute-start | bytes 2359304 | tf_op jit(solution)/shard_map/ppermute | solution.py:194
  172.3 1.6 copy-start.15
  173.9 2.0 copy-start.31
  173.9 2.0 copy-start.28
  173.9 2.8 copy-start.34
  197.5 28.4 %collective-permute-start.14 = (bf16[2,384,1024]{2,1,0:T(8,128)(2,1)}, bf16[2,384,1024]{2,1,0:T(8,128)(2,1)S(1)}, u32[]{:S(2)}, u32[]{:S(2)}) collective-permute-start(bf16[2,384,1024]{2,1,0:T(8,128)(2,1)} %get-tuple-element.39), channel_id=1, source_target_pairs={{0,4},{4,0},{8,12},{12,8},{16,20},{20,16},{24,28},{28,24},{1,5},{5... | collective-permute-start | bytes 4718600 | tf_op jit(solution)/shard_map/ppermute | solution.py:194
  197.6 25.9 %collective-permute-start.22 = (bf16[1024,512]{1,0:T(8,128)(2,1)}, bf16[1024,512]{1,0:T(8,128)(2,1)}, u32[]{:S(2)}, u32[]{:S(2)}) collective-permute-start(bf16[1024,512]{1,0:T(8,128)(2,1)} %convolution_convert_fusion), channel_id=1, source_target_pairs={{0,16},{4,20},{8,24},{12,28},{16,0},{20,4},{24,8},{28,12},{1,17},{... | collective-permute-start | bytes 3145736 | tf_op jit(solution)/shard_map/ppermute | solution.py:189
  199.1 5.5 %copy-start.8 = (bf16[2,384,1024]{2,1,0:T(8,128)(2,1)S(1)}, bf16[2,384,1024]{2,1,0:T(8,128)(2,1)}, u32[]{:S(2)}) copy-start(bf16[2,384,1024]{2,1,0:T(8,128)(2,1)} %add_convert_fusion.1) | copy-start | bytes 4718596
  199.1 24.3 %copy-start.16 = (bf16[768,1024]{1,0:T(8,128)(2,1)S(1)}, bf16[768,1024]{1,0:T(8,128)(2,1)}, u32[]{:S(2)}) copy-start(bf16[768,1024]{1,0:T(8,128)(2,1)} %copy-done.14) | copy-start | bytes 4718596
  199.1 24.3 %copy-start.32 = (bf16[768,1024]{1,0:T(8,128)(2,1)S(1)}, bf16[768,1024]{1,0:T(8,128)(2,1)}, u32[]{:S(2)}) copy-start(bf16[768,1024]{1,0:T(8,128)(2,1)} %copy-done.31) | copy-start | bytes 4718596
  202.2 23.6 %copy-start.19 = (f32[1024,512]{1,0:T(8,128)}, f32[1024,512]{1,0:T(8,128)S(1)}, u32[]{:S(2)}) copy-start(f32[1024,512]{1,0:T(8,128)S(1)} %convert_add_fusion.1) | copy-start | bytes 6291460
  203.2 62.3 %collective-permute-start.18 = (bf16[1024,256]{1,0:T(8,128)(2,1)}, bf16[1024,256]{1,0:T(8,128)(2,1)}, u32[]{:S(2)}, u32[]{:S(2)}) collective-permute-start(bf16[1024,256]{1,0:T(8,128)(2,1)} %dynamic-slice_convert_fusion.1), channel_id=1, source_target_pairs={{0,8},{4,12},{8,0},{12,4},{16,24},{20,28},{24,16},{28,20},{1,9},{5... | collective-permute-start | bytes 1572872 | tf_op jit(solution)/shard_map/ppermute | solution.py:189
  204.6 115.7 %collective-permute-start.16 = (bf16[2,384,1024]{2,1,0:T(8,128)(2,1)S(1)}, bf16[2,384,1024]{2,1,0:T(8,128)(2,1)}, u32[]{:S(2)}, u32[]{:S(2)}) collective-permute-start(bf16[2,384,1024]{2,1,0:T(8,128)(2,1)S(1)} %copy-done.8), channel_id=1, source_target_pairs={{8,0},{12,4},{16,8},{20,12},{24,16},{28,20},{9,1},{13,5},{17,9},{2... | collective-permute-start | bytes 4718600 | tf_op jit(solution)/shard_map/ppermute | solution.py:180
  223.4 2.4 copy-start.9
  225.8 3.7 %copy-start.17 = (f32[1024,512]{1,0:T(8,128)}, f32[1024,512]{1,0:T(8,128)S(1)}, u32[]{:S(2)}) copy-start(f32[1024,512]{1,0:T(8,128)S(1)} %convert_add_fusion) | copy-start | bytes 6291460
  225.9 2.4 copy-start.1
  228.2 97.7 %collective-permute-start.15 = (bf16[2,384,1024]{2,1,0:T(8,128)(2,1)}, bf16[2,384,1024]{2,1,0:T(8,128)(2,1)}, u32[]{:S(2)}, u32[]{:S(2)}) collective-permute-start(bf16[2,384,1024]{2,1,0:T(8,128)(2,1)} %add_convert_fusion), channel_id=1, source_target_pairs={{8,0},{12,4},{16,8},{20,12},{24,16},{28,20},{9,1},{13,5},{17,9},{2... | collective-permute-start | bytes 4718600 | tf_op jit(solution)/shard_map/ppermute | solution.py:180
  229.6 81.3 %collective-permute-start.23 = (bf16[1024,256]{1,0:T(8,128)(2,1)S(1)}, bf16[1024,256]{1,0:T(8,128)(2,1)S(1)}, u32[]{:S(2)}, u32[]{:S(2)}) collective-permute-start(bf16[1024,256]{1,0:T(8,128)(2,1)S(1)} %dynamic-slice_convert_fusion), channel_id=1, source_target_pairs={{0,8},{4,12},{8,0},{12,4},{16,24},{20,28},{24,16},{28,20},{1,9},{5... | collective-permute-start | bytes 1572872 | tf_op jit(solution)/shard_map/ppermute | solution.py:189
  265.5 46.5 %copy-start.18 = (f32[1024,512]{1,0:T(8,128)S(1)}, f32[1024,512]{1,0:T(8,128)}, u32[]{:S(2)}) copy-start(f32[1024,512]{1,0:T(8,128)} %copy-done.17) | copy-start | bytes 6291460
  267.2 45.7 %collective-permute-start.19 = (bf16[256,256]{1,0:T(8,128)(2,1)S(1)}, bf16[256,256]{1,0:T(8,128)(2,1)S(1)}, u32[]{:S(2)}, u32[]{:S(2)}) collective-permute-start(bf16[256,256]{1,0:T(8,128)(2,1)S(1)} %get-tuple-element.74), channel_id=1, source_target_pairs={{0,1},{1,2},{2,3},{3,0},{4,5},{5,6},{6,7},{7,4},{8,9},{9,10},{10,1... | collective-permute-start | bytes 393224 | tf_op jit(solution)/shard_map/ppermute | solution.py:185
  267.4 46.4 %collective-permute-start.20 = (bf16[256,256]{1,0:T(8,128)(2,1)S(1)}, bf16[256,256]{1,0:T(8,128)(2,1)S(1)}, u32[]{:S(2)}, u32[]{:S(2)}) collective-permute-start(bf16[256,256]{1,0:T(8,128)(2,1)S(1)} %get-tuple-element.76), channel_id=1, source_target_pairs={{0,2},{1,3},{2,0},{3,1},{4,6},{5,7},{6,4},{7,5},{8,10},{9,11},{10,... | collective-permute-start | bytes 393224 | tf_op jit(solution)/shard_map/ppermute | solution.py:185
  310.9 7.2 %collective-permute-start.21 = (bf16[256,256]{1,0:T(8,128)(2,1)S(1)}, bf16[256,256]{1,0:T(8,128)(2,1)S(1)}, u32[]{:S(2)}, u32[]{:S(2)}) collective-permute-start(bf16[256,256]{1,0:T(8,128)(2,1)S(1)} %get-tuple-element.75), channel_id=1, source_target_pairs={{0,3},{1,0},{2,1},{3,2},{4,7},{5,4},{6,5},{7,6},{8,11},{9,8},{10,9... | collective-permute-start | bytes 393224 | tf_op jit(solution)/shard_map/ppermute | solution.py:185
  312.9 11.8 %collective-permute-start.24 = (bf16[256,256]{1,0:T(8,128)(2,1)}, bf16[256,256]{1,0:T(8,128)(2,1)S(1)}, u32[]{:S(2)}, u32[]{:S(2)}) collective-permute-start(bf16[256,256]{1,0:T(8,128)(2,1)} %get-tuple-element.77), channel_id=1, source_target_pairs={{0,1},{1,2},{2,3},{3,0},{4,5},{5,6},{6,7},{7,4},{8,9},{9,10},{10,1... | collective-permute-start | bytes 393224 | tf_op jit(solution)/shard_map/ppermute | solution.py:185
  313.8 11.3 %collective-permute-start.25 = (bf16[256,256]{1,0:T(8,128)(2,1)S(1)}, bf16[256,256]{1,0:T(8,128)(2,1)S(1)}, u32[]{:S(2)}, u32[]{:S(2)}) collective-permute-start(bf16[256,256]{1,0:T(8,128)(2,1)S(1)} %get-tuple-element.79), channel_id=1, source_target_pairs={{0,2},{1,3},{2,0},{3,1},{4,6},{5,7},{6,4},{7,5},{8,10},{9,11},{10,... | collective-permute-start | bytes 393224 | tf_op jit(solution)/shard_map/ppermute | solution.py:185
  318.1 6.9 %collective-permute-start.26 = (bf16[256,256]{1,0:T(8,128)(2,1)S(1)}, bf16[256,256]{1,0:T(8,128)(2,1)S(1)}, u32[]{:S(2)}, u32[]{:S(2)}) collective-permute-start(bf16[256,256]{1,0:T(8,128)(2,1)S(1)} %get-tuple-element.78), channel_id=1, source_target_pairs={{0,3},{1,0},{2,1},{3,2},{4,7},{5,4},{6,5},{7,6},{8,11},{9,8},{10,9... | collective-permute-start | bytes 393224 | tf_op jit(solution)/shard_map/ppermute | solution.py:185
Sparse Core Ops, SparseCore 0:
  10.1 48.3 all-gather.2
  101.7 44.6 all-gather.4
